TPU v7x, 32 devices: a whole 2x2x4 slice. The times are simulated.
32 devices in a mesh: dp: 4 (over z), tp: 8 (over y, x, core).
Axes of the slice: x: 2, y: 2, z: 4, core: 2. Of those that a mesh axis runs over, the one named last changes fastest.
Arguments:
- hidden: bfloat16 [24, 128, 3584], P('dp', 'tp'), parts along dimension 0
- vision: bfloat16 [24, 2048, 3584], P('dp', 'tp'), parts along dimension 0
- positions: int32 [24, 128], P('dp', 'tp'), parts along dimension 0
- tile_mask: int32 [24, 128, 4], P('dp', 'tp'), parts along dimension 0
- ln1_a: bfloat16 [3584], replicated
- wq_a: bfloat16 [3584, 4096], P(None, 'tp')
- wk_a: bfloat16 [3584, 2048], P(None, 'tp')
- wv_a: bfloat16 [3584, 2048], P(None, 'tp')
- wo_a: bfloat16 [4096, 3584], P('tp')
- ln2_a: bfloat16 [3584], replicated
- wg_a: bfloat16 [3584, 14336], P(None, 'tp')
- wu_a: bfloat16 [3584, 14336], P(None, 'tp')
- wd_a: bfloat16 [14336, 3584], P('tp')
- ln1_b: bfloat16 [3584], replicated
- wq_b: bfloat16 [3584, 4096], P(None, 'tp')
- q_norm: bfloat16 [256], replicated
- wk_b: bfloat16 [3584, 2048], P(None, 'tp')
- wv_b: bfloat16 [3584, 2048], P(None, 'tp')
- k_norm: bfloat16 [256], replicated
- wo_b: bfloat16 [4096, 3584], P('tp')
- ln2_b: bfloat16 [3584], replicated
- wg_b: bfloat16 [3584, 14336], P(None, 'tp')
- wu_b: bfloat16 [3584, 14336], P(None, 'tp')
- wd_b: bfloat16 [14336, 3584], P('tp')
- xgates: float32 [2], replicated
Outputs:
- output: bfloat16 [24, 128, 3584], P('dp', 'tp'), parts along dimension 0
There are 4 independent parts. A program takes and returns all parts, laid end to end along the dimension named above; an argument that names none is the same for every part.
All inputs are finite; a program needn't handle non-finite values.
Results may differ from a plain program's by a relative error of at most 0.0163982.
Values are sent between devices in bfloat16 or wider.
A program may use at most 1 GiB of HBM per device.

v0:
```python
import math
import jax
import jax.numpy as jnp
from jax import lax
from jax.sharding import PartitionSpec as P

ROPE_THETA = 500000.0
ROPE_FACTOR = 8.0
LOW_FACTOR = 1.0
HIGH_FACTOR = 4.0
ORIG_CONTEXT = 8192.0
NORM_EPS = 1e-5
MASK_VALUE = -1e30


def rope_table(head_dim):
    low_wave = ORIG_CONTEXT / LOW_FACTOR
    high_wave = ORIG_CONTEXT / HIGH_FACTOR
    freq_list = []
    for freq_idx in range(head_dim // 2):
        base_freq = 1.0 / (ROPE_THETA ** (2.0 * freq_idx / head_dim))
        wave_len = 2.0 * math.pi / base_freq
        if wave_len > low_wave:
            freq_list.append(base_freq / ROPE_FACTOR)
        elif wave_len < high_wave:
            freq_list.append(base_freq)
        else:
            smooth = (ORIG_CONTEXT / wave_len - LOW_FACTOR) / (HIGH_FACTOR - LOW_FACTOR)
            freq_list.append((1.0 - smooth) * base_freq / ROPE_FACTOR + smooth * base_freq)
    return jnp.array(freq_list, dtype=jnp.float32)


def rms_scale(values, norm_gain):
    values = values.astype(jnp.float32)
    mean_sq = jnp.mean(values * values, axis=-1, keepdims=True)
    return values * lax.rsqrt(mean_sq + NORM_EPS) * norm_gain.astype(jnp.float32)


def rotate(values, cos_tab, sin_tab):
    half_dim = values.shape[-1] // 2
    first_half = values[..., :half_dim]
    second_half = values[..., half_dim:]
    return jnp.concatenate([first_half * cos_tab - second_half * sin_tab, second_half * cos_tab + first_half * sin_tab], axis=-1)


def self_attend(queries, key_vecs, val_vecs):
    seq_len = queries.shape[3]
    head_dim = queries.shape[4]
    scores = jnp.einsum('bgrtd,bsgd->bgrts', queries, key_vecs, preferred_element_type=jnp.float32) * (head_dim ** -0.5)
    causal = lax.broadcasted_iota(jnp.int32, (seq_len, seq_len), 0) >= lax.broadcasted_iota(jnp.int32, (seq_len, seq_len), 1)
    weights = jax.nn.softmax(jnp.where(causal, scores, MASK_VALUE), axis=-1).astype(jnp.bfloat16)
    return jnp.einsum('bgrts,bsgd->bgrtd', weights, val_vecs, preferred_element_type=jnp.float32).astype(jnp.bfloat16)


def cross_attend(queries, key_vecs, val_vecs, visible):
    batch_len, kv_groups, rep_heads, seq_len, head_dim = queries.shape
    vis_len = key_vecs.shape[1]
    tile_count = visible.shape[2]
    scores = jnp.einsum('bgrtd,bsgd->bgrts', queries, key_vecs, preferred_element_type=jnp.float32) * (head_dim ** -0.5)
    scores = scores.reshape(batch_len, kv_groups, rep_heads, seq_len, tile_count, vis_len // tile_count)
    scores = jnp.where(visible[:, None, None, :, :, None], scores, MASK_VALUE)
    weights = jax.nn.softmax(scores.reshape(batch_len, kv_groups, rep_heads, seq_len, vis_len), axis=-1).astype(jnp.bfloat16)
    return jnp.einsum('bgrts,bsgd->bgrtd', weights, val_vecs, preferred_element_type=jnp.float32).astype(jnp.bfloat16)


def gather_rows(values):
    return lax.all_gather(values, 'tp', axis=1, tiled=True)


def scatter_sum(partial):
    return lax.psum_scatter(partial, 'tp', scatter_dimension=1, tiled=True).astype(jnp.float32)


def gated_mlp(resid, norm_gain, w_gate, w_up, w_down):
    gathered = gather_rows(rms_scale(resid, norm_gain).astype(jnp.bfloat16))
    gate_proj = jnp.einsum('btd,df->btf', gathered, w_gate, preferred_element_type=jnp.float32)
    up_proj = jnp.einsum('btd,df->btf', gathered, w_up, preferred_element_type=jnp.float32)
    activated = (jax.nn.silu(gate_proj) * up_proj).astype(jnp.bfloat16)
    partial = jnp.einsum('btf,fd->btd', activated, w_down, preferred_element_type=jnp.float32).astype(jnp.bfloat16)
    return scatter_sum(partial)


def solution(mesh):
    act_spec = P('dp', 'tp', None)
    col_spec = P(None, 'tp')
    row_spec = P('tp', None)
    layer_a = (P(), col_spec, col_spec, col_spec, row_spec, P(), col_spec, col_spec, row_spec)
    layer_b = (P(), col_spec, P(), col_spec, col_spec, P(), row_spec, P(), col_spec, col_spec, row_spec, P())
    in_specs = (act_spec, act_spec, P('dp', 'tp'), act_spec) + layer_a + layer_b

    def body(hidden, vision, positions, tile_mask, ln1_a, wq_a, wk_a, wv_a, wo_a, ln2_a, wg_a, wu_a, wd_a, ln1_b, wq_b, q_norm, wk_b, wv_b, k_norm, wo_b, ln2_b, wg_b, wu_b, wd_b, xgates):
        head_dim = q_norm.shape[0]
        model_dim = hidden.shape[2]
        kv_local = wk_a.shape[1] // head_dim
        rep_heads = wq_a.shape[1] // head_dim // kv_local
        query_shape = (model_dim, kv_local, rep_heads, head_dim)
        head_shape = (model_dim, kv_local, head_dim)
        out_shape = (kv_local, rep_heads, head_dim, model_dim)
        angles = gather_rows(positions).astype(jnp.float32)[..., None] * rope_table(head_dim)
        cos_tab = jnp.cos(angles)
        sin_tab = jnp.sin(angles)
        gathered = gather_rows(rms_scale(hidden, ln1_a).astype(jnp.bfloat16))
        queries = jnp.einsum('btd,dgre->bgrte', gathered, wq_a.reshape(query_shape), preferred_element_type=jnp.float32)
        queries = rotate(queries, cos_tab[:, None, None], sin_tab[:, None, None]).astype(jnp.bfloat16)
        key_vecs = jnp.einsum('btd,dge->btge', gathered, wk_a.reshape(head_shape), preferred_element_type=jnp.float32)
        key_vecs = rotate(key_vecs, cos_tab[:, :, None], sin_tab[:, :, None]).astype(jnp.bfloat16)
        val_vecs = jnp.einsum('btd,dge->btge', gathered, wv_a.reshape(head_shape), preferred_element_type=jnp.float32).astype(jnp.bfloat16)
        context = self_attend(queries, key_vecs, val_vecs)
        partial = jnp.einsum('bgrtd,grde->bte', context, wo_a.reshape(out_shape), preferred_element_type=jnp.float32).astype(jnp.bfloat16)
        h_one = (hidden.astype(jnp.float32) + scatter_sum(partial)).astype(jnp.bfloat16)
        h_two = (h_one.astype(jnp.float32) + gated_mlp(h_one, ln2_a, wg_a, wu_a, wd_a)).astype(jnp.bfloat16)
        gathered = gather_rows(rms_scale(h_two, ln1_b).astype(jnp.bfloat16))
        queries = jnp.einsum('btd,dgre->bgrte', gathered, wq_b.reshape(query_shape), preferred_element_type=jnp.float32)
        queries = rms_scale(queries, q_norm).astype(jnp.bfloat16)
        vis_full = gather_rows(vision)
        key_vecs = jnp.einsum('bsd,dge->bsge', vis_full, wk_b.reshape(head_shape), preferred_element_type=jnp.float32)
        key_vecs = rms_scale(key_vecs, k_norm).astype(jnp.bfloat16)
        val_vecs = jnp.einsum('bsd,dge->bsge', vis_full, wv_b.reshape(head_shape), preferred_element_type=jnp.float32).astype(jnp.bfloat16)
        context = cross_attend(queries, key_vecs, val_vecs, gather_rows(tile_mask) > 0)
        partial = jnp.einsum('bgrtd,grde->bte', context, wo_b.reshape(out_shape), preferred_element_type=jnp.float32).astype(jnp.bfloat16)
        row_keep = jnp.any(tile_mask > 0, axis=-1, keepdims=True).astype(jnp.float32)
        gate_vals = jnp.tanh(xgates.astype(jnp.float32))
        h_three = (h_two.astype(jnp.float32) + gate_vals[0] * row_keep * scatter_sum(partial)).astype(jnp.bfloat16)
        mlp_out = gated_mlp(h_three, ln2_b, wg_b, wu_b, wd_b)
        return (h_three.astype(jnp.float32) + gate_vals[1] * row_keep * mlp_out).astype(jnp.bfloat16)

    return jax.shard_map(body, mesh=mesh, in_specs=in_specs, out_specs=act_spec, check_vma=False)
```

profile of v0, /device:TPU:0, one launch (start us, length us, event | category | flops | bytes accessed | tf_op | source)
XLA Modules:
  0.0 1063.1 jit_solution(9861979737721308133)
XLA Ops:
  6.5 1.4 fusion.68
  8.0 0.7 convert_element_type.134
  8.7 2.2 fusion.70
  11.0 10.7 %all-gather = s32[8,16,6]{1,2,0:T(8,128)S(1)} all-gather(s32[1,16,6]{1,2,0:T(8,128)} %bitcast.198), channel_id=1, replica_groups=mesh['dp'=4,'tp'=8] {'tp'}, dimensions={0}, use_global_device_ids=true | all-gather | bytes 3456 | tf_op jit(solution)/shard_map/all_gather | solution.py:67
  21.7 2.1 multiply_cosine_fusion.1
  23.8 31.8 %all-gather.7.cloned.1.call-done = bf16[6,128,3584]{2,1,0:T(8,128)(2,1)} async-done(((bf16[6,16,3584]{2,1,0:T(8,128)(2,1)}), bf16[6,128,3584]{2,1,0:T(8,128)(2,1)}) %all-gather.7.cloned.1.call-update) | async-done | bytes 5505040 | tf_op jit(solution)/shard_map/all_gather | solution.py:67
  55.6 4.9 fusion.84
  60.5 2.5 fusion.117
  63.0 3.0 fusion.59
  66.2 1.5 fusion.135
  67.7 4.7 fusion.92
  72.4 7.2 bitcast_convert_fusion.1
  79.7 0.6 copy-done.9
  80.3 56.7 %reduce-scatter.5.cloned.1.call-done = bf16[6,16,3584]{2,1,0:T(8,128)(2,1)} async-done(((bf16[6,128,3584]{2,1,0:T(8,128)(2,1)}), bf16[6,16,3584]{2,1,0:T(8,128)(2,1)}) %reduce-scatter.5.cloned.1.call-update) | async-done | bytes 688144 | tf_op jit(solution)/shard_map/reduce_scatter | solution.py:71
  137.0 1.4 fusion.72
  138.4 1.1 fusion.74
  139.5 0.5 reduce-scatter.7.cloned.1.call-start
  140.0 41.5 %all-gather.9.cloned.1.call-done = bf16[6,128,3584]{2,1,0:T(8,128)(2,1)} async-done(((bf16[6,16,3584]{2,1,0:T(8,128)(2,1)}), bf16[6,128,3584]{2,1,0:T(8,128)(2,1)}) %all-gather.9.cloned.1.call-update) | async-done | bytes 5505040 | tf_op jit(solution)/shard_map/all_gather | solution.py:67
  181.5 16.3 %fusion.12 = f32[6,128,1792]{2,1,0:T(8,128)} fusion(bf16[6,128,3584]{2,1,0:T(8,128)(2,1)} %all-gather.9.cloned.1.call-done, bf16[3584,1792]{1,0:T(8,128)(2,1)} %param.36), kind=kOutput, calls=%fused_computation.12 | convolution fusion | flops 9865003008 | bytes 23855104 | tf_op jit(solution)/shard_map/btd,df->btf/dot_general | solution.py:76
  197.8 33.5 %fusion.15 = bf16[6,128,3584]{2,1,0:T(8,128)(2,1)} fusion(bf16[1792,3584]{1,0:T(8,128)(2,1)} %param.38, f32[6,128,1792]{2,1,0:T(8,128)} %fusion.12, bf16[6,128,3584]{2,1,0:T(8,128)(2,1)} %all-gather.9.cloned.1.call-done, bf16[3584,1792]{1,0:T(8,128)(2,1)} %param.37), kind=kOutput, calls=%fused_computation.22 | convolution fusion | flops 19741016064 | bytes 42205184 | tf_op jit(solution)/shard_map/btf,fd->btd/dot_general | solution.py:79
  231.4 0.6 copy-done.10
  232.1 56.7 %reduce-scatter.7.cloned.1.call-done = bf16[6,16,3584]{2,1,0:T(8,128)(2,1)} async-done(((bf16[6,128,3584]{2,1,0:T(8,128)(2,1)}), bf16[6,16,3584]{2,1,0:T(8,128)(2,1)}) %reduce-scatter.7.cloned.1.call-update) | async-done | bytes 688144 | tf_op jit(solution)/shard_map/reduce_scatter | solution.py:71
  288.8 1.4 fusion.76
  290.2 2.2 fusion.78
  292.5 0.5 all-gather.13.cloned.1.call-update
  293.3 9.4 all_gather.24
  303.1 1.2 broadcast_in_dim.22
  304.2 3.7 broadcast_in_dim.23
  307.9 26.5 %all-gather.11.cloned.1.call-done = bf16[6,128,3584]{2,1,0:T(8,128)(2,1)} async-done(((bf16[6,16,3584]{2,1,0:T(8,128)(2,1)}), bf16[6,128,3584]{2,1,0:T(8,128)(2,1)}) %all-gather.11.cloned.1.call-update) | async-done | bytes 5505040 | tf_op jit(solution)/shard_map/all_gather | solution.py:67
  334.4 6.2 fusion.56
  340.6 387.2 %all-gather.13.cloned.1.call-done = bf16[6,2048,3584]{2,1,0:T(8,128)(2,1)} async-done(((bf16[6,256,3584]{2,1,0:T(8,128)(2,1)}), bf16[6,2048,3584]{2,1,0:T(8,128)(2,1)}) %all-gather.13.cloned.1.call-update) | async-done | bytes 88080400 | tf_op jit(solution)/shard_map/all_gather | solution.py:67
  727.9 40.5 %multiply_reduce_fusion = (f32[6,2048]{1,0:T(8,128)S(1)}, f32[6,2048,256]{1,2,0:T(8,128)}) fusion(bf16[6,2048,3584]{2,1,0:T(8,128)(2,1)} %all-gather.13.cloned.1.call-done, bf16[3584,256]{1,0:T(8,128)(2,1)S(1)} %copy-done), kind=kOutput, calls=%fused_computation.18 | convolution fusion | flops 22554857472 | bytes 102547456 | tf_op jit(solution)/shard_map/bsd,dge->bsge/dot_general | solution.py:116
  768.4 11.3 %fusion.22 = f32[6,2,128,2048]{3,2,1,0:T(8,128)} fusion(f32[6,2048,256]{1,2,0:T(8,128)} %get-tuple-element.20, f32[256]{0:T(256)S(1)} %convert_element_type.155, f32[6,2048]{1,0:T(8,128)S(1)} %add_rsqrt_fusion, f32[6,128,2,256]{3,1,2,0:T(8,128)S(1)} %get-tuple-element.24, f32[256]{0:T(256)S(1)} %convert_element_type.153, f32[6,2,128]{2,1,0:T(2,128)S(1)} %add_rsqrt_fusion.1), kind=kOutput, calls=%fused_computation.25 | convolution fusion | flops 1621229568 | bytes 26796032 | tf_op jit(solution)/shard_map/bgrtd,bsgd->bgrts/dot_general | solution.py:59
  779.7 16.2 %fusion.138 = (f32[6,2,128]{2,1,0:T(2,128)S(1)}, f32[6,2,128,2048]{3,2,1,0:T(8,128)}) fusion(f32[6,2,128,2048]{3,2,1,0:T(8,128)} %fusion.22, pred[6,128,2048]{2,1,0:T(8,128)(4,1)S(1)} %copy-done.6), kind=kOutput, calls=%fused_computation.147 | output fusion | flops 18876416 | bytes 26744832 | tf_op jit(solution)/shard_map/sub | solution.py:62
  795.9 35.2 %fusion.162 = bf16[6,2048,256,1]{2,1,3,0:T(8,128)(2,1)} fusion(bf16[6,2048,3584]{2,1,0:T(8,128)(2,1)} %all-gather.13.cloned.1.call-done, bf16[3584,256]{1,0:T(8,128)(2,1)} %param.43), kind=kOutput, calls=%fused_computation.27.clone.clone.clone.2 | convolution fusion | flops 22551724032 | bytes 96206848 | tf_op jit(solution)/shard_map/bsd,dge->bsge/dot_general | solution.py:118
  831.0 8.4 fusion.63
  839.4 4.8 bitcast_convert_fusion
  844.4 0.6 copy-done.18
  845.0 0.6 fusion.134
  845.6 1.3 broadcast_select_fusion
  846.9 54.8 %reduce-scatter.9.cloned.1.call-done = bf16[6,16,3584]{2,1,0:T(8,128)(2,1)} async-done(((bf16[6,128,3584]{2,1,0:T(8,128)(2,1)}), bf16[6,16,3584]{2,1,0:T(8,128)(2,1)}) %reduce-scatter.9.cloned.1.call-update) | async-done | bytes 688144 | tf_op jit(solution)/shard_map/reduce_scatter | solution.py:71
  901.7 1.6 fusion.80
  903.3 1.1 fusion.82
  904.4 41.9 %all-gather.15.cloned.1.call-done = bf16[6,128,3584]{2,1,0:T(8,128)(2,1)} async-done(((bf16[6,16,3584]{2,1,0:T(8,128)(2,1)}), bf16[6,128,3584]{2,1,0:T(8,128)(2,1)}) %all-gather.15.cloned.1.call-update) | async-done | bytes 5505040 | tf_op jit(solution)/shard_map/all_gather | solution.py:67
  946.3 16.5 %fusion.6 = f32[6,128,1792]{2,1,0:T(8,128)} fusion(bf16[6,128,3584]{2,1,0:T(8,128)(2,1)} %all-gather.15.cloned.1.call-done, bf16[3584,1792]{1,0:T(8,128)(2,1)} %param.47), kind=kOutput, calls=%fused_computation.6 | convolution fusion | flops 9865003008 | bytes 23855104 | tf_op jit(solution)/shard_map/btd,df->btf/dot_general | solution.py:76
  962.9 33.7 %fusion.18 = bf16[6,128,3584]{2,1,0:T(8,128)(2,1)} fusion(bf16[1792,3584]{1,0:T(8,128)(2,1)} %param.49, f32[6,128,1792]{2,1,0:T(8,128)} %fusion.6, bf16[6,128,3584]{2,1,0:T(8,128)(2,1)} %all-gather.15.cloned.1.call-done, bf16[3584,1792]{1,0:T(8,128)(2,1)} %param.48), kind=kOutput, calls=%fused_computation.23 | convolution fusion | flops 19741016064 | bytes 42205184 | tf_op jit(solution)/shard_map/btf,fd->btd/dot_general | solution.py:79
  996.6 57.4 %reduce-scatter.11.cloned.1.call-done = bf16[6,16,3584]{2,1,0:T(8,128)(2,1)} async-done(((bf16[6,128,3584]{2,1,0:T(8,128)(2,1)}), bf16[6,16,3584]{2,1,0:T(8,128)(2,1)}) %reduce-scatter.11.cloned.1.call-update) | async-done | bytes 688144 | tf_op jit(solution)/shard_map/reduce_scatter | solution.py:71
  1054.0 2.2 fusion.83
  (72 shorter events, 1.5 us)
Async XLA Ops:
  6.5 721.3 %copy-start = (bf16[3584,256]{1,0:T(8,128)(2,1)S(1)}, bf16[3584,256]{1,0:T(8,128)(2,1)}, u32[]{:S(2)}) copy-start(bf16[3584,256]{1,0:T(8,128)(2,1)} %param.42) | copy-start | bytes 5505028
  6.5 49.1 %all-gather.7.cloned.1.call-start = ((), (), s32[]{:S(2)}) async-start(), calls=%async_computation.4 | async-start | bytes 6193152 | tf_op jit(solution)/shard_map/all_gather | solution.py:67
  10.9 49.6 %copy-start.12 = (f32[128]{0:T(128)S(1)}, f32[128]{0:T(128)}, u32[]{:S(2)}) copy-start(f32[128]{0:T(128)} %constant.38.clone) | copy-start | bytes 1540
  10.9 126.1 %reduce-scatter.5.cloned.1.call-start = ((), (), s32[]{:S(2)}) async-start(), calls=%async_computation.5 | async-start | bytes 6193152 | tf_op jit(solution)/shard_map/reduce_scatter | solution.py:71
  55.6 7.3 copy-start.13
  55.6 7.3 copy-start.14
  79.6 0.7 copy-start.9
  79.6 57.4 %copy-start.4 = (bf16[6,16,3584]{2,1,0:T(8,128)(2,1)S(1)}, bf16[6,16,3584]{2,1,0:T(8,128)(2,1)}, u32[]{:S(2)}) copy-start(bf16[6,16,3584]{2,1,0:T(8,128)(2,1)} %param.26) | copy-start | bytes 2064388
  79.6 101.9 %all-gather.9.cloned.1.call-start = ((), (), s32[]{:S(2)}) async-start(), calls=%async_computation.6 | async-start | bytes 6193152 | tf_op jit(solution)/shard_map/all_gather | solution.py:67
  138.4 151.8 %copy-start.2 = (bf16[6,16,3584]{2,1,0:T(8,128)(2,1)}, bf16[6,16,3584]{2,1,0:T(8,128)(2,1)S(1)}, u32[]{:S(2)}) copy-start(bf16[6,16,3584]{2,1,0:T(8,128)(2,1)S(1)} %get-tuple-element.8) | copy-start | bytes 2064388
  139.5 149.2 %reduce-scatter.7.cloned.1.call-start = ((), (), s32[]{:S(2)}) async-start(), calls=%async_computation.7 | async-start | bytes 6193152 | tf_op jit(solution)/shard_map/reduce_scatter | solution.py:71
  231.4 0.7 copy-start.10
  231.4 103.0 %all-gather.11.cloned.1.call-start = ((), (), s32[]{:S(2)}) async-start(), calls=%async_computation.8 | async-start | bytes 6193152 | tf_op jit(solution)/shard_map/all_gather | solution.py:67
  292.4 0.7 copy-start.16
  292.4 0.7 copy-start.17
  292.5 0.7 copy-start.7
  292.5 435.4 %all-gather.13.cloned.1.call-start = ((), (), s32[]{:S(2)}) async-start(), calls=%async_computation.9 | async-start | bytes 99090432 | tf_op jit(solution)/shard_map/all_gather | solution.py:67
  293.0 608.6 %reduce-scatter.9.cloned.1.call-start = ((), (), s32[]{:S(2)}) async-start(), calls=%async_computation.10 | async-start | bytes 6193152 | tf_op jit(solution)/shard_map/reduce_scatter | solution.py:71
  768.4 11.3 %copy-start.6 = (pred[6,128,2048]{2,1,0:T(8,128)(4,1)S(1)}, pred[6,128,2048]{2,1,0:T(8,128)(4,1)}, u32[]{:S(2)}) copy-start(pred[6,128,2048]{2,1,0:T(8,128)(4,1)} %broadcast_in_dim.23) | copy-start | bytes 4718596
  831.0 8.4 copy-start.15
  844.3 0.7 copy-start.18
  844.3 0.7 copy-start.11
  844.3 1.3 copy-start.8
  844.3 57.4 %copy-start.3 = (bf16[6,16,3584]{2,1,0:T(8,128)(2,1)S(1)}, bf16[6,16,3584]{2,1,0:T(8,128)(2,1)}, u32[]{:S(2)}) copy-start(bf16[6,16,3584]{2,1,0:T(8,128)(2,1)} %copy-done.2) | copy-start | bytes 2064388
  844.3 57.4 %copy-start.5 = (bf16[6,16,3584]{2,1,0:T(8,128)(2,1)S(1)}, bf16[6,16,3584]{2,1,0:T(8,128)(2,1)}, u32[]{:S(2)}) copy-start(bf16[6,16,3584]{2,1,0:T(8,128)(2,1)} %reduce-scatter.7.cloned.1.call-done) | copy-start | bytes 2064388
  844.3 102.0 %all-gather.15.cloned.1.call-start = ((), (), s32[]{:S(2)}) async-start(), calls=%async_computation.11 | async-start | bytes 6193152 | tf_op jit(solution)/shard_map/all_gather | solution.py:67
  904.4 149.6 %reduce-scatter.11.cloned.1.call-start = ((), (), s32[]{:S(2)}) async-start(), calls=%async_computation.12 | async-start | bytes 6193152 | tf_op jit(solution)/shard_map/reduce_scatter | solution.py:71
  962.9 93.3 %copy-start.1 = (bf16[3584,256]{1,0:T(8,128)(2,1)S(1)}, bf16[3584,256]{1,0:T(8,128)(2,1)}, u32[]{:S(2)}) copy-start(bf16[3584,256]{1,0:T(8,128)(2,1)} %param.42) | copy-start | bytes 5505028
Sparse Core Ops, SparseCore 0:
  11.0 44.5 all-gather.6
  79.8 57.1 reduce-scatter.4
  139.6 41.8 all-gather.8
  231.5 57.2 reduce-scatter.6
  292.5 41.7 all-gather.10
  336.2 391.6 all-gather.12
  844.4 57.2 reduce-scatter.8
  904.5 41.7 all-gather.14
  996.7 57.2 reduce-scatter.10
where the time goes:
time: 1070 us; the launch traced here: 1060 us
  waiting for transfers between devices  755 us (71%)
  matrix products  228 us (21%)
  other arithmetic  37.7 us (4%)
  blocking collectives  20.1 us (2%)
  between operations  13.9 us (1%)
    all_gather x5, waiting for transfers between devices, gather_rows(): return lax.all_gather(values, 'tp', axis=1, tiled=True)  529 us
    reduce_scatter x4, waiting for transfers between devices, scatter_sum(): lax.psum_scatter(partial, 'tp', scatter_dimension=1, tiled=True)  226 us
    dot_general x2, matrix products, gated_mlp(): jnp.einsum('btf,fd->btd', activated, w_down, preferred_element_type=jnp.f...  67.2 us
    dot_general x1, matrix products, body(): jnp.einsum('bsd,dge->bsge', vis_full, wk_b.reshape(head_shape), preferred...  40.5 us
    dot_general x1, matrix products, body(): jnp.einsum('bsd,dge->bsge', vis_full, wv_b.reshape(head_shape), preferred...  35.2 us
    dot_general x2, matrix products, gated_mlp(): jnp.einsum('btd,df->btf', gathered, w_gate, preferred_element_type=jnp.fl...  32.8 us
  transfers between devices with their start and end apart: 9, of which 9 were waited for; matrix products, arithmetic and copies ran while one was open for 1% of the time, Pallas kernels for 0%

commit v1 on v0

v1 whole, which is shorter than its diff:
```python
import functools
import math
import jax
import jax.numpy as jnp
from jax import lax
from jax.experimental import pallas as pl
from jax.experimental.pallas import tpu as pltpu
from jax.sharding import PartitionSpec as P

ROPE_THETA = 500000.0
ROPE_FACTOR = 8.0
LOW_FACTOR = 1.0
HIGH_FACTOR = 4.0
ORIG_CONTEXT = 8192.0
NORM_EPS = 1e-5
MASK_VALUE = -1e30


def rope_table(head_dim):
    low_wave = ORIG_CONTEXT / LOW_FACTOR
    high_wave = ORIG_CONTEXT / HIGH_FACTOR
    freq_list = []
    for freq_idx in range(head_dim // 2):
        base_freq = 1.0 / (ROPE_THETA ** (2.0 * freq_idx / head_dim))
        wave_len = 2.0 * math.pi / base_freq
        if wave_len > low_wave:
            freq_list.append(base_freq / ROPE_FACTOR)
        elif wave_len < high_wave:
            freq_list.append(base_freq)
        else:
            smooth = (ORIG_CONTEXT / wave_len - LOW_FACTOR) / (HIGH_FACTOR - LOW_FACTOR)
            freq_list.append((1.0 - smooth) * base_freq / ROPE_FACTOR + smooth * base_freq)
    return jnp.array(freq_list, dtype=jnp.float32)


def rms_scale(values, norm_gain):
    values = values.astype(jnp.float32)
    mean_sq = jnp.mean(values * values, axis=-1, keepdims=True)
    return values * lax.rsqrt(mean_sq + NORM_EPS) * norm_gain.astype(jnp.float32)


def rotate(values, cos_tab, sin_tab):
    half_dim = values.shape[-1] // 2
    first_half = values[..., :half_dim]
    second_half = values[..., half_dim:]
    return jnp.concatenate([first_half * cos_tab - second_half * sin_tab, second_half * cos_tab + first_half * sin_tab], axis=-1)


def self_attend(queries, key_vecs, val_vecs):
    seq_len = queries.shape[3]
    head_dim = queries.shape[4]
    scores = jnp.einsum('bgrtd,bsgd->bgrts', queries, key_vecs, preferred_element_type=jnp.float32) * (head_dim ** -0.5)
    causal = lax.broadcasted_iota(jnp.int32, (seq_len, seq_len), 0) >= lax.broadcasted_iota(jnp.int32, (seq_len, seq_len), 1)
    weights = jax.nn.softmax(jnp.where(causal, scores, MASK_VALUE), axis=-1).astype(jnp.bfloat16)
    return jnp.einsum('bgrts,bsgd->bgrtd', weights, val_vecs, preferred_element_type=jnp.float32).astype(jnp.bfloat16)


def cross_attend(queries, key_vecs, val_vecs, visible):
    batch_len, kv_groups, rep_heads, seq_len, head_dim = queries.shape
    vis_len = key_vecs.shape[1]
    tile_count = visible.shape[2]
    scores = jnp.einsum('bgrtd,bsgd->bgrts', queries, key_vecs, preferred_element_type=jnp.float32) * (head_dim ** -0.5)
    scores = scores.reshape(batch_len, kv_groups, rep_heads, seq_len, tile_count, vis_len // tile_count)
    scores = jnp.where(visible[:, None, None, :, :, None], scores, MASK_VALUE)
    weights = jax.nn.softmax(scores.reshape(batch_len, kv_groups, rep_heads, seq_len, vis_len), axis=-1).astype(jnp.bfloat16)
    return jnp.einsum('bgrts,bsgd->bgrtd', weights, val_vecs, preferred_element_type=jnp.float32).astype(jnp.bfloat16)


MESH = pl.DeviceIdType.MESH
D_SUM, X_ONE, Y_ONE, Y_TWO, X_TWO, X_OWN, Y_OWN, C_OWN, Y_FWD, X_FWD, C_X, C_Y, C_DIAG = range(13)
FLOWS = 13
TILE = 256


def fused_kernel(samples, has_pre, has_post, swiglu, gated, has_aux, n_post, *refs):
    refs = list(refs)
    take = lambda n: [refs.pop(0) for _ in range(n)]
    lhs, w_pre = take(2) if has_pre else (None, None)
    resid, = take(1)
    gate, = take(1) if gated else (None,)
    gain, = take(1) if has_post else (None,)
    w_post = take(n_post)
    aux, = take(1) if has_aux else (None,)
    h_out, = take(1) if has_pre else (None,)
    res, = take(1) if has_post else (None,)
    aux_out, = take(1) if has_aux else (None,)
    if has_pre:
        wv_pre, part, rec_d, acc, rec_x1, rec_y1, two_l, two_h, rec_y2, rec_x2 = take(10)
    wv_post = take(n_post)
    out, = take(1) if has_post else (None,)
    send, recv, wsem = take(3)
    me = lax.axis_index('tp')
    c = me % 2
    x = (me // 2) % 2
    y = me // 4
    pc, px, py = me + 1 - 2 * c, me + 2 - 4 * x, me + 4 - 8 * y
    rows, dim = resid.shape[1:]
    half = dim // 2
    lo, hi = pl.ds(0, half), pl.ds(half, half)

    loads = []
    if has_pre:
        loads.append(pltpu.make_async_copy(w_pre, wv_pre, wsem.at[0]))
    for i in range(n_post):
        loads.append(pltpu.make_async_copy(w_post[i], wv_post[i], wsem.at[1 + i]))
    for ld in loads:
        ld.start()

    def slot(s, dy, dx, dc):
        return out.at[s, (1 - y) if dy else y, (1 - x) if dx else x, (1 - c) if dc else c]

    def ends(flow, s):
        if flow == D_SUM:
            return part.at[s, :, :, 1 - c], rec_d.at[s], pc, rec_d.at[s]
        if flow == X_ONE:
            return acc.at[s, :, 1 - x, :, lo], rec_x1.at[s], px, rec_x1.at[s]
        if flow == Y_ONE:
            return acc.at[s, 1 - y, :, :, hi], rec_y1.at[s], py, rec_y1.at[s]
        if flow == Y_TWO:
            return two_l.at[s, 1 - y], rec_y2.at[s], py, rec_y2.at[s]
        if flow == X_TWO:
            return two_h.at[s, 1 - x], rec_x2.at[s], px, rec_x2.at[s]
        own, sx, sy, sd = slot(s, 0, 0, 0), slot(s, 0, 1, 0), slot(s, 1, 0, 0), slot(s, 1, 1, 0)
        if flow == X_OWN:
            return own, own, px, sx
        if flow == Y_OWN:
            return own, own, py, sy
        if flow == C_OWN:
            return own, own, pc, slot(s, 0, 0, 1)
        if flow == Y_FWD:
            return sx.at[:, lo], sx.at[:, lo], py, sd.at[:, lo]
        if flow == X_FWD:
            return sy.at[:, hi], sy.at[:, hi], px, sd.at[:, hi]
        if flow == C_X:
            return sx, sx, pc, slot(s, 0, 1, 1)
        if flow == C_Y:
            return sy, sy, pc, slot(s, 1, 0, 1)
        return sd, sd, pc, slot(s, 1, 1, 1)

    def descr(flow, s, incoming):
        src, dst, who, landing = ends(flow, s)
        return pltpu.make_async_remote_copy(src_ref=src, dst_ref=landing if incoming else dst, send_sem=send.at[flow, s], recv_sem=recv.at[flow, s], device_id={'tp': who}, device_id_type=MESH)

    def start(flow, s):
        descr(flow, s, False).start()

    def got(flow, s):
        descr(flow, s, True).wait_recv()

    def f32(value):
        return value.astype(jnp.float32)

    def normed(values):
        mean_sq = jnp.mean(values * values, axis=-1, keepdims=True)
        return (values * lax.rsqrt(mean_sq + NORM_EPS) * f32(gain[...])).astype(jnp.bfloat16)

    barrier = pltpu.get_barrier_semaphore()
    peers = [lax.rem(me + k, 8) for k in range(1, 8)] if has_aux else [pc, px, py]
    for who in peers:
        pl.semaphore_signal(barrier, inc=1, device_id={'tp': who}, device_id_type=MESH)
    pl.semaphore_wait(barrier, len(peers))

    aux_sent = []
    if has_aux:
        aux_send, aux_recv = take(2)
        aux_out[me] = aux[...]
        for k in range(1, 8):
            cp = pltpu.make_async_remote_copy(src_ref=aux, dst_ref=aux_out.at[me], send_sem=aux_send.at[k], recv_sem=aux_recv.at[k], device_id={'tp': lax.rem(me + k, 8)}, device_id_type=MESH)
            cp.start()
            aux_sent.append(cp)

    def st_pre(s):
        @pl.when(s == 0)
        def _():
            loads[0].wait()
        left = lhs[s]
        for n in range(dim // TILE):
            cols = pl.ds(n * TILE, TILE)
            prod = jnp.dot(left, wv_pre[:, cols], preferred_element_type=jnp.float32)
            part[s, :, :, :, :, cols] = prod.astype(jnp.bfloat16).reshape(2, 2, 2, rows, TILE)
        start(D_SUM, s)

    def st_r1(s):
        got(D_SUM, s)
        acc[s] = (f32(part[s, :, :, c]) + f32(rec_d[s])).astype(jnp.bfloat16)
        start(X_ONE, s)
        start(Y_ONE, s)

    def st_r2(s):
        got(X_ONE, s)
        two_l[s] = (f32(acc[s, :, x, :, lo]) + f32(rec_x1[s])).astype(jnp.bfloat16)
        start(Y_TWO, s)
        got(Y_ONE, s)
        two_h[s] = (f32(acc[s, y, :, :, hi]) + f32(rec_y1[s])).astype(jnp.bfloat16)
        start(X_TWO, s)

    def st_r3(s):
        got(Y_TWO, s)
        got(X_TWO, s)
        total = jnp.concatenate([f32(two_l[s, y]) + f32(rec_y2[s]), f32(two_h[s, x]) + f32(rec_x2[s])], axis=-1)
        if gated:
            total = total * gate[s]
        new = (f32(resid[s]) + total).astype(jnp.bfloat16)
        h_out[s] = new
        if has_post:
            out[s, y, x, c] = normed(f32(new))
            for flow in (X_OWN, Y_OWN, C_OWN):
                start(flow, s)

    def st_g1(s):
        out[s, y, x, c] = normed(f32(resid[s]))
        for flow in (X_OWN, Y_OWN, C_OWN):
            start(flow, s)

    def st_g2(s):
        got(X_OWN, s)
        start(Y_FWD, s)
        start(C_X, s)
        got(Y_OWN, s)
        start(X_FWD, s)
        start(C_Y, s)

    def st_g3(s):
        got(Y_FWD, s)
        got(X_FWD, s)
        start(C_DIAG, s)

    def st_g4(s):
        for flow in (C_OWN, C_X, C_Y, C_DIAG):
            got(flow, s)

        @pl.when(s == 0)
        def _():
            for ld in loads[len(loads) - n_post:]:
                ld.wait()
        left = out[s].reshape(8 * rows, dim)
        if swiglu:
            for n in range(res.shape[-1] // TILE):
                cols = pl.ds(n * TILE, TILE)
                gate_proj = jnp.dot(left, wv_post[0][:, cols], preferred_element_type=jnp.float32)
                up_proj = jnp.dot(left, wv_post[1][:, cols], preferred_element_type=jnp.float32)
                res[s, :, cols] = (jax.nn.silu(gate_proj) * up_proj).astype(jnp.bfloat16)
        else:
            base = 0
            for w in wv_post:
                for n in range(w.shape[-1] // TILE):
                    res[s, :, pl.ds(base, TILE)] = jnp.dot(left, w[:, pl.ds(n * TILE, TILE)], preferred_element_type=jnp.float32)
                    base += TILE

    flows, stages = [], []
    if has_pre:
        stages += [st_pre, st_r1, st_r2, st_r3]
        flows += [D_SUM, X_ONE, Y_ONE, Y_TWO, X_TWO]
    else:
        stages += [st_g1]
    if has_post:
        stages += [st_g2, st_g3, st_g4]
        flows += [X_OWN, Y_OWN, C_OWN, Y_FWD, X_FWD, C_X, C_Y, C_DIAG]

    def step(t, carry):
        for k, stage in enumerate(stages):
            s = t - k

            @pl.when((s >= 0) & (s < samples))
            def _(stage=stage, s=s):
                stage(s)
        return carry

    lax.fori_loop(0, samples + len(stages) - 1, step, 0)

    def drain(s, carry):
        for flow in flows:
            descr(flow, s, False).wait_send()
        return carry

    lax.fori_loop(0, samples, drain, 0)
    for k in range(1, 8 if has_aux else 1):
        src = lax.rem(me + 8 - k, 8)
        pltpu.make_async_remote_copy(src_ref=aux, dst_ref=aux_out.at[src], send_sem=aux_send.at[k], recv_sem=aux_recv.at[k], device_id={'tp': pc}, device_id_type=MESH).wait_recv()
    for cp in aux_sent:
        cp.wait_send()


def fused(cid, resid, lhs=None, w_pre=None, gate=None, gain=None, w_post=(), swiglu=False, aux=None):
    samples, rows, dim = resid.shape
    bf16 = jnp.bfloat16
    half = dim // 2
    has_pre, has_post = lhs is not None, gain is not None
    vmem = pl.BlockSpec(memory_space=pltpu.VMEM)
    hbm = pl.BlockSpec(memory_space=pl.ANY)
    args, specs, outs, scratch = [], [], [], []

    def add(value, spec):
        args.append(value)
        specs.append(spec)

    flops = 0
    if has_pre:
        add(lhs, vmem)
        add(w_pre, hbm)
        flops += 2 * samples * 8 * rows * w_pre.size
        outs.append(jax.ShapeDtypeStruct(resid.shape, bf16))
        scratch += [
            pltpu.VMEM(w_pre.shape, bf16),
            pltpu.VMEM((samples, 2, 2, 2, rows, dim), bf16),
            pltpu.VMEM((samples, 2, 2, rows, dim), bf16), pltpu.VMEM((samples, 2, 2, rows, dim), bf16),
            pltpu.VMEM((samples, 2, rows, half), bf16), pltpu.VMEM((samples, 2, rows, half), bf16),
            pltpu.VMEM((samples, 2, rows, half), bf16), pltpu.VMEM((samples, 2, rows, half), bf16),
            pltpu.VMEM((samples, rows, half), bf16), pltpu.VMEM((samples, rows, half), bf16)]
    add(resid, vmem)
    if gate is not None:
        add(gate, vmem)
    if has_post:
        add(gain.reshape(1, dim), vmem)
        for w in w_post:
            add(w, hbm)
            flops += 2 * samples * 8 * rows * w.size
            scratch.append(pltpu.VMEM(w.shape, bf16))
        if swiglu:
            outs.append(jax.ShapeDtypeStruct((samples, 8 * rows, w_post[0].shape[1]), bf16))
        else:
            outs.append(jax.ShapeDtypeStruct((samples, 8 * rows, sum(w.shape[1] for w in w_post)), jnp.float32))
        scratch.append(pltpu.VMEM((samples, 2, 2, 2, rows, dim), bf16))
    if aux is not None:
        add(aux, vmem)
        outs.append(jax.ShapeDtypeStruct((8,) + aux.shape, aux.dtype))
    scratch += [pltpu.SemaphoreType.DMA((FLOWS, samples)), pltpu.SemaphoreType.DMA((FLOWS, samples)), pltpu.SemaphoreType.DMA((1 + len(w_post),))]
    if aux is not None:
        scratch += [pltpu.SemaphoreType.DMA((8,)), pltpu.SemaphoreType.DMA((8,))]
    return pl.pallas_call(
        functools.partial(fused_kernel, samples, has_pre, has_post, swiglu, gate is not None, aux is not None, len(w_post)),
        out_shape=tuple(outs), in_specs=specs, out_specs=tuple([vmem] * len(outs)),
        scratch_shapes=scratch, name=f'fused_{cid}',
        cost_estimate=pl.CostEstimate(flops=flops + 2 * 10 ** 10, bytes_accessed=10 ** 7, transcendentals=0),
        compiler_params=pltpu.CompilerParams(collective_id=cid, has_side_effects=True, vmem_limit_bytes=67043328),
    )(*args)


Q_X, Q_Y, Q_YF, Q_XF, O_X1, O_Y1, O_Y2, O_X2 = range(8)
STAT = 8


def cross_kernel(samples, q_ref, k_hbm, v_hbm, vis_ref, ctx, q_all, k_vm, v_vm, ob_l, ob_h, rec_x1, rec_y1, two_l, two_h, rec_y2, rec_x2, send, recv, ksem):
    me = lax.axis_index('tp')
    x = (me // 2) % 2
    y = me // 4
    px, py = me + 2 - 4 * x, me + 4 - 8 * y
    rows, size = q_ref.shape[1:]
    top, low = pl.ds(0, rows // 2), pl.ds(rows // 2, rows // 2)
    half = size // 2
    scale = size ** -0.5
    loads = [pltpu.make_async_copy(k_hbm, k_vm, ksem.at[0]), pltpu.make_async_copy(v_hbm, v_vm, ksem.at[1])]
    for ld in loads:
        ld.start()

    def ends(flow, s):
        own, sx, sy, sd = q_all.at[s, y, x], q_all.at[s, y, 1 - x], q_all.at[s, 1 - y, x], q_all.at[s, 1 - y, 1 - x]
        if flow == Q_X:
            return own, own, px, sx
        if flow == Q_Y:
            return own, own, py, sy
        if flow == Q_YF:
            return sx.at[top], sx.at[top], py, sd.at[top]
        if flow == Q_XF:
            return sy.at[low], sy.at[low], px, sd.at[low]
        if flow == O_X1:
            return ob_l.at[s, :, 1 - x], rec_x1.at[s], px, rec_x1.at[s]
        if flow == O_Y1:
            return ob_h.at[s, 1 - y], rec_y1.at[s], py, rec_y1.at[s]
        if flow == O_Y2:
            return two_l.at[s, 1 - y], rec_y2.at[s], py, rec_y2.at[s]
        return two_h.at[s, 1 - x], rec_x2.at[s], px, rec_x2.at[s]

    def descr(flow, s, incoming):
        src, dst, who, landing = ends(flow, s)
        return pltpu.make_async_remote_copy(src_ref=src, dst_ref=landing if incoming else dst, send_sem=send.at[flow, s], recv_sem=recv.at[flow, s], device_id={'tp': who}, device_id_type=MESH)

    def start(flow, s):
        descr(flow, s, False).start()

    def got(flow, s):
        descr(flow, s, True).wait_recv()

    barrier = pltpu.get_barrier_semaphore()
    for who in (px, py):
        pl.semaphore_signal(barrier, inc=1, device_id={'tp': who}, device_id_type=MESH)
    pl.semaphore_wait(barrier, 2)

    def stat_block(top_row, sum_row):
        return jnp.concatenate([top_row, sum_row] + [top_row] * (STAT - 2), axis=0)

    def merged(a, b):
        max_a, max_b = a[half:half + 1], b[half:half + 1]
        peak = jnp.maximum(max_a, max_b)
        fac_a, fac_b = jnp.exp(max_a - peak), jnp.exp(max_b - peak)
        total = a[half + 1:half + 2] * fac_a + b[half + 1:half + 2] * fac_b
        return a[:half] * fac_a + b[:half] * fac_b, peak, total

    def st_a(s):
        q_all[s, y, x] = q_ref[s]
        start(Q_X, s)
        start(Q_Y, s)

    def st_b(s):
        got(Q_X, s)
        start(Q_YF, s)
        got(Q_Y, s)
        start(Q_XF, s)

    def st_c(s):
        got(Q_YF, s)
        got(Q_XF, s)

        @pl.when(s == 0)
        def _():
            for ld in loads:
                ld.wait()
        seen = vis_ref[s] > 0
        for p in range(4):
            cols = pl.ds(p * size, size)
            keys = k_vm[:, s, :, cols].reshape(-1, size)
            vals = v_vm[:, s, :, cols].reshape(-1, size)
            scores = lax.dot_general(keys, q_all[s, p // 2, p % 2], (((1,), (1,)), ((), ())), preferred_element_type=jnp.float32) * scale
            scores = jnp.where(seen, scores, MASK_VALUE)
            peak = jnp.max(scores, axis=0, keepdims=True)
            weights = jnp.exp(scores - peak)
            total = jnp.sum(weights, axis=0, keepdims=True)
            context = lax.dot_general(vals, weights.astype(jnp.bfloat16), (((0,), (0,)), ((), ())), preferred_element_type=jnp.float32)
            stats = stat_block(peak, total)
            ob_l[s, p // 2, p % 2, :half] = context[:half]
            ob_h[s, p // 2, p % 2, :half] = context[half:]
            ob_l[s, p // 2, p % 2, half:] = stats
            ob_h[s, p // 2, p % 2, half:] = stats
        start(O_X1, s)
        start(O_Y1, s)

    def st_d(s):
        got(O_X1, s)
        for q in range(2):
            body, peak, total = merged(ob_l[s, q, x], rec_x1[s, q])
            two_l[s, q, :half] = body
            two_l[s, q, half:] = stat_block(peak, total)
        start(O_Y2, s)
        got(O_Y1, s)
        for q in range(2):
            body, peak, total = merged(ob_h[s, y, q], rec_y1[s, q])
            two_h[s, q, :half] = body
            two_h[s, q, half:] = stat_block(peak, total)
        start(O_X2, s)

    def st_e(s):
        got(O_Y2, s)
        got(O_X2, s)
        parts = []
        for mine, other in ((two_l[s, y], rec_y2[s]), (two_h[s, x], rec_x2[s])):
            body, _, total = merged(mine, other)
            parts.append(body / total)
        whole = jnp.concatenate(parts, axis=0).T.astype(jnp.bfloat16)
        reps = rows // ctx.shape[1]
        for r in range(reps):
            ctx[s, :, r * size:(r + 1) * size] = whole[r * ctx.shape[1]:(r + 1) * ctx.shape[1]]

    stages = [st_a, st_b, st_c, st_d, st_e]

    def step(t, carry):
        for k, stage in enumerate(stages):
            s = t - k

            @pl.when((s >= 0) & (s < samples))
            def _(stage=stage, s=s):
                stage(s)
        return carry

    lax.fori_loop(0, samples + len(stages) - 1, step, 0)

    def drain(s, carry):
        for flow in range(8):
            descr(flow, s, False).wait_send()
        return carry

    lax.fori_loop(0, samples, drain, 0)


def cross(cid, queries, keys, vals, seen, tokens):
    samples, rows, size = queries.shape
    f32, bf16 = jnp.float32, jnp.bfloat16
    half = size // 2
    vmem = pl.BlockSpec(memory_space=pltpu.VMEM)
    hbm = pl.BlockSpec(memory_space=pl.ANY)
    wide = pltpu.VMEM((samples, 2, half + STAT, rows), f32)
    one = pltpu.VMEM((samples, half + STAT, rows), f32)
    both = pltpu.VMEM((samples, 2, 2, half + STAT, rows), f32)
    return pl.pallas_call(
        functools.partial(cross_kernel, samples),
        out_shape=jax.ShapeDtypeStruct((samples, tokens, rows // tokens * size), bf16),
        in_specs=[vmem, hbm, hbm, vmem], out_specs=vmem,
        scratch_shapes=[
            pltpu.VMEM((samples, 2, 2, rows, size), bf16), pltpu.VMEM(keys.shape, bf16), pltpu.VMEM(vals.shape, bf16),
            both, both, wide, wide, wide, wide, one, one,
            pltpu.SemaphoreType.DMA((8, samples)), pltpu.SemaphoreType.DMA((8, samples)), pltpu.SemaphoreType.DMA((2,))],
        name=f'cross_{cid}',
        cost_estimate=pl.CostEstimate(flops=5 * 10 ** 10, bytes_accessed=10 ** 7, transcendentals=0),
        compiler_params=pltpu.CompilerParams(collective_id=cid, has_side_effects=True, vmem_limit_bytes=60 * 2 ** 20),
    )(queries, keys, vals, seen)


def kv_kernel(head_dim, own_ref, par_ref, wk_ref, wv_ref, gain_ref, k_ref, v_ref):
    for i, src in enumerate((own_ref, par_ref)):
        rows = src[0]
        for n in range(wk_ref.shape[1] // head_dim):
            cols = pl.ds(n * head_dim, head_dim)
            keys = jnp.dot(rows, wk_ref[:, cols], preferred_element_type=jnp.float32)
            mean_sq = jnp.mean(keys * keys, axis=-1, keepdims=True)
            k_ref[i, 0, :, cols] = (keys * lax.rsqrt(mean_sq + NORM_EPS) * gain_ref[...].astype(jnp.float32)).astype(jnp.bfloat16)
            v_ref[i, 0, :, cols] = jnp.dot(rows, wv_ref[:, cols], preferred_element_type=jnp.float32).astype(jnp.bfloat16)


def project_kv(own, partner, wk, wv, gain):
    samples, rows, dim = own.shape
    width = wk.shape[1]
    rows_spec = pl.BlockSpec((1, rows, dim), lambda s: (s, 0, 0))
    weight_spec = pl.BlockSpec((dim, width), lambda s: (0, 0))
    out_spec = pl.BlockSpec((2, 1, rows, width), lambda s: (0, s, 0, 0))
    out = jax.ShapeDtypeStruct((2, samples, rows, width), jnp.bfloat16)
    return pl.pallas_call(
        functools.partial(kv_kernel, gain.shape[0]), grid=(samples,),
        in_specs=[rows_spec, rows_spec, weight_spec, weight_spec, pl.BlockSpec((1, gain.shape[0]), lambda s: (0, 0))],
        out_specs=(out_spec, out_spec), out_shape=(out, out), name='project_kv',
        cost_estimate=pl.CostEstimate(flops=8 * samples * rows * dim * width, bytes_accessed=10 ** 8, transcendentals=0),
        compiler_params=pltpu.CompilerParams(vmem_limit_bytes=60 * 2 ** 20),
    )(own, partner, wk, wv, gain.reshape(1, -1))


def solution(mesh):
    act_spec = P('dp', 'tp', None)
    col_spec = P(None, 'tp')
    row_spec = P('tp', None)
    layer_a = (P(), col_spec, col_spec, col_spec, row_spec, P(), col_spec, col_spec, row_spec)
    layer_b = (P(), col_spec, P(), col_spec, col_spec, P(), row_spec, P(), col_spec, col_spec, row_spec, P())
    in_specs = (act_spec, act_spec, P('dp', 'tp'), act_spec) + layer_a + layer_b

    def body(hidden, vision, positions, tile_mask, ln1_a, wq_a, wk_a, wv_a, wo_a, ln2_a, wg_a, wu_a, wd_a, ln1_b, wq_b, q_norm, wk_b, wv_b, k_norm, wo_b, ln2_b, wg_b, wu_b, wd_b, xgates):
        me = lax.axis_index('tp')
        head_dim = q_norm.shape[0]
        samples, rows, model_dim = hidden.shape
        tokens = rows * 8
        tiles = tile_mask.shape[2]
        kv_local = wk_a.shape[1] // head_dim
        rep_heads = wq_a.shape[1] // head_dim // kv_local

        same_core = [[core + 2 * chip for chip in range(4)] for core in range(2)]
        wk_all = lax.all_gather(wk_b, 'tp', axis=1, tiled=True, axis_index_groups=same_core)
        wv_all = lax.all_gather(wv_b, 'tp', axis=1, tiled=True, axis_index_groups=same_core)
        vis_partner = lax.ppermute(vision, 'tp', [(i, i ^ 1) for i in range(8)])

        small = jnp.concatenate([positions.reshape(-1), tile_mask.reshape(-1)])
        aux = jnp.pad(small, (0, 1024 - small.shape[0])).reshape(8, 128)
        proj, aux_all = fused(1, hidden, gain=ln1_a, w_post=(wq_a, wk_a, wv_a), aux=aux)
        aux_all = aux_all.reshape(8, 1024)
        pos_all = aux_all[:, :samples * rows].reshape(8, samples, rows).transpose(1, 0, 2).reshape(samples, tokens)
        mask_all = aux_all[:, samples * rows:samples * rows * (1 + tiles)].reshape(8, samples, rows, tiles).transpose(1, 0, 2, 3).reshape(samples, tokens, tiles)

        angles = pos_all.astype(jnp.float32)[..., None] * rope_table(head_dim)
        cos_tab = jnp.cos(angles)[:, :, None, :]
        sin_tab = jnp.sin(angles)[:, :, None, :]
        proj = proj.reshape(samples, tokens, rep_heads + 2, head_dim)
        rotated = rotate(proj[:, :, :rep_heads + 1], cos_tab, sin_tab).astype(jnp.bfloat16)
        queries = rotated[:, :, :rep_heads].transpose(0, 2, 1, 3)[:, None]
        context = self_attend(queries, rotated[:, :, rep_heads:], proj[:, :, rep_heads + 1:].astype(jnp.bfloat16))
        context = context[:, 0].transpose(0, 2, 1, 3).reshape(samples, tokens, rep_heads * head_dim)
        h_one, act = fused(2, hidden, lhs=context, w_pre=wo_a, gain=ln2_a, w_post=(wg_a, wu_a), swiglu=True)
        h_two, queries = fused(3, h_one, lhs=act, w_pre=wd_a, gain=ln1_b, w_post=(wq_b,))
        queries = rms_scale(queries.reshape(samples, tokens, rep_heads, head_dim), q_norm).astype(jnp.bfloat16)
        queries = queries.transpose(0, 2, 1, 3).reshape(samples, rep_heads * tokens, head_dim)
        keys, vals = project_kv(vision, vis_partner, wk_all, wv_all, k_norm)
        seen = jnp.tile(lax.dynamic_index_in_dim(mask_all, me // 2, axis=2, keepdims=False)[:, None, :], (1, 1, rep_heads))
        context = cross(6, queries, keys, vals, seen, tokens)
        row_keep = jnp.any(tile_mask > 0, axis=-1, keepdims=True).astype(jnp.float32)
        gate_vals = jnp.tanh(xgates.astype(jnp.float32))
        h_three, act = fused(4, h_two, lhs=context, w_pre=wo_b, gate=gate_vals[0] * row_keep, gain=ln2_b, w_post=(wg_b, wu_b), swiglu=True)
        return fused(5, h_three, lhs=act, w_pre=wd_b, gate=gate_vals[1] * row_keep)[0]

    return jax.shard_map(body, mesh=mesh, in_specs=in_specs, out_specs=act_spec, check_vma=False)
```

time: 1070 us -> 530 us (0.50)
  waiting for transfers between devices: 755 us -> 0.83 us
  Pallas kernels: 0 us -> 488 us
  matrix products: 228 us -> 0.85 us
  other arithmetic: 37.7 us -> 5.37 us
  blocking collectives: 20.1 us -> 0 us
  local copies, waits for them, and re-layouts: 7.9 us -> 20.4 us
    all_gather x5 -> x2, waiting for transfers between devices: 529 us -> 0.01 us  [the longest x1 0.01 us: body(): lax.all_gather(wk_b, 'tp', axis=1, tiled=True, axis_index_groups=same_core)]
    pallas_call x0 -> x7, Pallas kernels: none -> 488 us  [the longest x5 348 us: fused(): pl.pallas_call(functools.partial(fused_kernel, samples, has_pre, has_post...]
    reduce_scatter x4 -> x0, waiting for transfers between devices: 226 us -> none  [scatter_sum(): lax.psum_scatter(partial, 'tp', scatter_dimension=1, tiled=True)]
    dot_general x14 -> x2, matrix products: 226 us -> 0.85 us  [the longest x1 0.46 us: self_attend(): jnp.einsum('bgrts,bsgd->bgrtd', weights, val_vecs, preferred_element_type...]
    all_gather x2 -> x0, blocking collectives: 20.1 us -> none  [gather_rows(): return lax.all_gather(values, 'tp', axis=1, tiled=True)]
    sub x1, other arithmetic: 16.2 us -> 0.18 us  [self_attend(): jax.nn.softmax(jnp.where(causal, scores, MASK_VALUE), axis=-1)]
  transfers between devices with their start and end apart: 9 -> 3, of which waited for: 9 -> 0; matrix products, arithmetic and copies ran while one was open for 1% -> 4% of each run, Pallas kernels for 0% -> 46%
where the time goes in v1:
time: 530 us
  Pallas kernels  488 us (92%)
  local copies, waits for them, and re-layouts  20.4 us (4%)
  between operations  13.8 us (3%)
  other arithmetic  5.37 us (1%)
    pallas_call x5, Pallas kernels, fused(): pl.pallas_call(functools.partial(fused_kernel, samples, has_pre, has_post...  348 us
    pallas_call x1, Pallas kernels, cross(): pl.pallas_call(functools.partial(cross_kernel, samples), out_shape=jax.Sh...  85.3 us
    pallas_call x1, Pallas kernels, project_kv(): pl.pallas_call(functools.partial(kv_kernel, gain.shape[0]), grid=(samples...  54.8 us
  transfers between devices with their start and end apart: 3, of which 0 were waited for; matrix products, arithmetic and copies ran while one was open for 4% of the time, Pallas kernels for 46%

profile of v1, /device:TPU:0, one launch (start us, length us, event | category | flops | bytes accessed | tf_op | source)
XLA Modules:
  0.0 529.9 jit_solution(12518790551585186017)
XLA Ops:
  6.5 0.7 all-gather.3.cloned.1.call-update
  7.3 0.0 all-gather.5.cloned.1.call-start
  7.3 0.6 collective-permute-start
  7.9 0.1 all-gather.5.cloned.1.call-update
  8.0 0.1 copy.62
  8.1 0.1 reshape.128
  8.3 0.1 reshape.127
  8.3 0.1 pad_add_fusion
  8.4 0.6 pad_bitcast_fusion.refs_5_
  9.0 0.6 reshape.126.refs_1_
  9.6 51.9 %fused_1.1 = (f32[6,128,1024]{2,1,0:T(8,128)}, s32[8,8,128]{2,1,0:T(8,128)}) custom-call(bf16[6,16,3584]{2,1,0:T(8,128)(2,1)} %refs_2_.3, bf16[1,3584]{1,0:T(2,128)(2,1)} %reshape.126.refs_1_, bf16[3584,512]{1,0:T(8,128)(2,1)} %refs_2_.2, bf16[3584,256]{1,0:T(8,128)(2,1)} %refs_3_.1, bf16[3584,256]{1,0:T(8,128)(2,1)} %refs_4_.3, ...), custom_call_target="tpu_custom_call" | custom-call | flops 25637144576 | bytes 10000000 | tf_op jit(solution)/shard_map/fused_1/pallas_call | solution.py:330
  61.6 3.4 reshape.130
  65.0 0.7 slice.46
  65.7 0.1 convert_element_type.38
  65.8 0.1 convert_element_type.40
  65.9 1.7 slice.45
  67.6 1.4 multiply_cosine_fusion
  69.0 0.7 fusion.17
  69.8 0.3 add_convert_fusion
  70.1 0.4 fusion.4
  70.5 0.2 fusion.19
  70.7 0.5 copy-done
  71.3 0.5 fusion.2
  71.7 1.0 copy.86
  72.7 0.6 reshape.135.refs_3_
  73.3 0.6 reshape.136.refs_3_
  73.9 94.0 %fused_2.1 = (bf16[6,16,3584]{2,1,0:T(8,128)(2,1)}, bf16[6,128,1792]{2,1,0:T(8,128)(2,1)}) custom-call(bf16[6,128,512]{2,1,0:T(8,128)(2,1)} %bitcast.52, bf16[512,3584]{1,0:T(8,128)(2,1)} %refs_1_.4, bf16[6,16,3584]{2,1,0:T(8,128)(2,1)} %refs_2_.3, bf16[1,3584]{1,0:T(2,128)(2,1)} %reshape.135.refs_3_, bf16[3584,1792]{1,0:T(8,128)(2,1)} %refs_4_.4, ...), custom_call_target="tpu_custom_call" | custom-call | flops 42548576256 | bytes 10000000 | tf_op jit(solution)/shard_map/fused_2/pallas_call | solution.py:330
  167.9 98.2 %fused_3.1 = (bf16[6,16,3584]{2,1,0:T(8,128)(2,1)}, f32[6,128,512]{2,1,0:T(8,128)}) custom-call(bf16[6,128,1792]{2,1,0:T(8,128)(2,1)} %get-tuple-element.17.refs_0_, bf16[1792,3584]{1,0:T(8,128)(2,1)} %refs_1_.5, bf16[6,16,3584]{2,1,0:T(8,128)(2,1)} %get-tuple-element.18.refs_2_, bf16[1,3584]{1,0:T(2,128)(2,1)} %reshape.136.refs_3_, bf16[3584,512]{1,0:T(8,128)(2,1)} %refs_4_.5), custom_call_target="tpu_custom_call" | custom-call | flops 32683575296 | bytes 10000000 | tf_op jit(solution)/shard_map/fused_3/pallas_call | solution.py:330
  266.1 2.3 reshape.137
  268.4 0.9 multiply_reduce_fusion
  269.3 0.1 add_rsqrt_fusion
  269.4 1.0 fusion.7
  270.5 1.0 copy.72
  271.5 0.1 copy.81
  271.6 0.1 copy.74
  271.7 0.1 reshape.141
  271.9 0.5 reshape.139.gain_ref
  272.5 0.6 fusion.18
  273.1 1.3 select_bitcast_fusion
  274.4 0.7 copy.75.refs_3_
  275.2 0.6 reshape.142.refs_4_
  275.8 0.7 copy.76.refs_3_
  276.5 54.8 %project_kv.1 = (bf16[2,6,256,1024]{3,2,1,0:T(8,128)(2,1)}, bf16[2,6,256,1024]{3,2,1,0:T(8,128)(2,1)}) custom-call(bf16[6,256,3584]{2,1,0:T(8,128)(2,1)} %own_ref.1, bf16[6,256,3584]{2,1,0:T(8,128)(2,1)} %collective-permute-done.par_ref, bf16[3584,1024]{1,0:T(8,128)(2,1)} %all-gather.3.cloned.1.call-done.wk_ref, ...), custom_call_target="tpu_custom_call" | custom-call | flops 45097156608 | bytes 100000000 | tf_op jit(solution)/shard_map/project_kv/pallas_call | solution.py:525
  331.3 0.6 tile.11
  331.9 85.3 %cross_6.1.refs_0_ = bf16[6,128,512]{2,1,0:T(8,128)(2,1)} custom-call(bf16[6,256,256]{2,1,0:T(8,128)(2,1)} %bitcast.51, bf16[2,6,256,1024]{3,2,1,0:T(8,128)(2,1)} %get-tuple-element.20.k_hbm, bf16[2,6,256,1024]{3,2,1,0:T(8,128)(2,1)} %get-tuple-element.21.v_hbm, s32[6,1,256]{2,1,0:T(1,128)} %bitcast.59), custom_call_target="tpu_custom_call" | custom-call | flops 49999998976 | bytes 10000000 | tf_op jit(solution)/shard_map/cross_6/pallas_call | solution.py:493
  417.3 65.6 %fused_4.1 = (bf16[6,16,3584]{2,1,0:T(8,128)(2,1)}, bf16[6,128,1792]{2,1,0:T(8,128)(2,1)}) custom-call(bf16[6,128,512]{2,1,0:T(8,128)(2,1)} %cross_6.1.refs_0_, bf16[512,3584]{1,0:T(8,128)(2,1)} %refs_1_.6, bf16[6,16,3584]{2,1,0:T(8,128)(2,1)} %get-tuple-element.22.refs_2_, f32[6,16,1]{2,1,0:T(8,128)} %copy.75.refs_3_, bf16[1,3584]{1,0:T(2,128)(2,1)} %reshape.142.refs_4_, ...), custom_call_target="tpu_custom_call" | custom-call | flops 42548576256 | bytes 10000000 | tf_op jit(solution)/shard_map/fused_4/pallas_call | solution.py:330
  482.9 38.2 %fused_5.1 = bf16[6,16,3584]{2,1,0:T(8,128)(2,1)} custom-call(bf16[6,128,1792]{2,1,0:T(8,128)(2,1)} %get-tuple-element.23.refs_0_, bf16[1792,3584]{1,0:T(8,128)(2,1)} %refs_1_.7, bf16[6,16,3584]{2,1,0:T(8,128)(2,1)} %get-tuple-element.24.refs_2_, f32[6,16,1]{2,1,0:T(8,128)} %copy.76.refs_3_), custom_call_target="tpu_custom_call" | custom-call | flops 29865003008 | bytes 10000000 | tf_op jit(solution)/shard_map/fused_5/pallas_call | solution.py:330
  521.1 2.0 copy.104
  (40 shorter events, 0.2 us)
Async XLA Ops:
  6.5 1.5 copy-start.2
  6.5 1.7 copy-start.9
  6.5 2.5 copy-start.5
  6.5 270.0 %all-gather.3.cloned.1.call-start = ((), (), s32[]{:S(2)}) async-start(), calls=%async_computation | async-start | bytes 9175040 | tf_op jit(solution)/shard_map/all_gather | solution.py:552
  7.3 269.2 %all-gather.5.cloned.1.call-start = ((), (), s32[]{:S(2)}) async-start(), calls=%async_computation.1 | async-start | bytes 9175040 | tf_op jit(solution)/shard_map/all_gather | solution.py:553
  7.3 269.2 %collective-permute-start = (bf16[6,256,3584]{2,1,0:T(8,128)(2,1)}, bf16[6,256,3584]{2,1,0:T(8,128)(2,1)}, u32[]{:S(2)}, u32[]{:S(2)}) collective-permute-start(bf16[6,256,3584]{2,1,0:T(8,128)(2,1)} %own_ref.1), channel_id=1, source_target_pairs={{0,1},{1,0},{2,3},{3,2},{4,5},{5,4},{6,7},{7,6},{8,9},{9,8},{10,11... | collective-permute-start | bytes 33030152 | tf_op jit(solution)/shard_map/ppermute | solution.py:554
  61.5 3.5 copy-start.4
  65.0 2.6 copy-start.10
  70.1 1.1 copy-start
  71.7 1.0 copy-start.6
  71.7 1.6 copy-start.7
  266.1 2.3 copy-start.11
  269.4 2.1 copy-start.1
  270.4 1.5 copy-start.12
  270.4 2.0 copy-start.13
  270.4 2.6 copy-start.3
  270.5 4.7 copy-start.8
Sparse Core Ops, SparseCore 0:
  9.2 120.9 all-gather.2
  132.0 120.7 all-gather.4

commit v2 on v1

--- a/solution.py
+++ b/solution.py
@@ -70,30 +70,41 @@
 D_SUM, X_ONE, Y_ONE, Y_TWO, X_TWO, X_OWN, Y_OWN, C_OWN, Y_FWD, X_FWD, C_X, C_Y, C_DIAG = range(13)
 FLOWS = 13
 TILE = 256
-
-
-def fused_kernel(samples, has_pre, has_post, swiglu, gated, has_aux, n_post, *refs):
+CHUNK = 112
+
+
+def fused_kernel(samples, has_pre, has_post, mode, gated, has_aux, has_attn, n_post, gain_row, near_part, has_far, *refs):
     refs = list(refs)
     take = lambda n: [refs.pop(0) for _ in range(n)]
     lhs, w_pre = take(2) if has_pre else (None, None)
+    cos, sin = take(2) if has_attn else (None, None)
+    q_gain, = take(1) if mode == 'queries' else (None,)
     resid, = take(1)
     gate, = take(1) if gated else (None,)
     gain, = take(1) if has_post else (None,)
     w_post = take(n_post)
     aux, = take(1) if has_aux else (None,)
+    own_w = take(2) if near_part is not None else None
+    far_src, = take(1) if has_far else (None,)
     h_out, = take(1) if has_pre else (None,)
     res, = take(1) if has_post else (None,)
     aux_out, = take(1) if has_aux else (None,)
+    near_out, = take(1) if near_part is not None else (None,)
+    far_out, = take(1) if has_far else (None,)
     if has_pre:
         wv_pre, part, rec_d, acc, rec_x1, rec_y1, two_l, two_h, rec_y2, rec_x2 = take(10)
     wv_post = take(n_post)
     out, = take(1) if has_post else (None,)
     send, recv, wsem = take(3)
+    near_send, near_recv, fwd_send, fwd_recv = take(4) if near_part is not None else (None,) * 4
+    far_send, far_recv = take(2) if has_far else (None, None)
     me = lax.axis_index('tp')
     c = me % 2
     x = (me // 2) % 2
     y = me // 4
     pc, px, py = me + 1 - 2 * c, me + 2 - 4 * x, me + 4 - 8 * y
+    z = lax.axis_index('dp')
+    pz = z + 1 - 2 * (z % 2)
     rows, dim = resid.shape[1:]
     half = dim // 2
     lo, hi = pl.ds(0, half), pl.ds(half, half)
@@ -152,13 +163,45 @@
 
     def normed(values):
         mean_sq = jnp.mean(values * values, axis=-1, keepdims=True)
-        return (values * lax.rsqrt(mean_sq + NORM_EPS) * f32(gain[...])).astype(jnp.bfloat16)
+        return (values * lax.rsqrt(mean_sq + NORM_EPS) * f32(gain[gain_row:gain_row + 1])).astype(jnp.bfloat16)
 
     barrier = pltpu.get_barrier_semaphore()
     peers = [lax.rem(me + k, 8) for k in range(1, 8)] if has_aux else [pc, px, py]
     for who in peers:
         pl.semaphore_signal(barrier, inc=1, device_id={'tp': who}, device_id_type=MESH)
-    pl.semaphore_wait(barrier, len(peers))
+    if has_far:
+        pl.semaphore_signal(barrier, inc=1, device_id={'dp': pz}, device_id_type=MESH)
+    pl.semaphore_wait(barrier, len(peers) + (1 if has_far else 0))
+
+    part_rows = near_out.shape[2] if near_part is not None else 0
+    chunks = part_rows // CHUNK
+
+    def near_copy(p, kind, j):
+        first = part_rows * (2 * near_part + z % 2) + j * CHUNK
+        return pltpu.make_async_remote_copy(src_ref=own_w[kind].at[pl.ds(pl.multiple_of(first, CHUNK), CHUNK)], dst_ref=near_out.at[p, kind, pl.ds(j * CHUNK, CHUNK)], send_sem=near_send.at[p, kind, j], recv_sem=near_recv.at[p, kind, j], device_id={'tp': (px, py)[p]}, device_id_type=MESH)
+
+    def fwd_copy(p, j):
+        span = pl.ds(j * CHUNK, CHUNK)
+        return pltpu.make_async_remote_copy(src_ref=near_out.at[p, :, span], dst_ref=near_out.at[2, :, span], send_sem=fwd_send.at[j], recv_sem=fwd_recv.at[j], device_id={'tp': (py, px)[p]}, device_id_type=MESH)
+
+    def chunk_send(j):
+        for p in range(2):
+            for kind in range(2):
+                near_copy(p, kind, j).start()
+
+    def chunk_forward(j):
+        for p in range(2):
+            for kind in range(2):
+                near_copy(p, kind, j).wait_recv()
+        for p in range(2):
+            @pl.when(j % 2 == p)
+            def _(p=p):
+                fwd_copy(p, j).start()
+
+    far_copy = None
+    if has_far:
+        far_copy = pltpu.make_async_remote_copy(src_ref=far_src, dst_ref=far_out, send_sem=far_send, recv_sem=far_recv, device_id={'dp': pz}, device_id_type=MESH)
+        far_copy.start()
 
     aux_sent = []
     if has_aux:
@@ -169,11 +212,33 @@
             cp.start()
             aux_sent.append(cp)
 
+    def self_attention(s):
+        size = 2 * cos.shape[-1]
+        heads = lhs.shape[-1] // size - 2
+        cos_tab, sin_tab = cos[s], sin[s]
+
+        def head(i):
+            return lhs[s, :, i * size:(i + 1) * size]
+
+        keys = rotate(head(heads), cos_tab, sin_tab).astype(jnp.bfloat16)
+        vals = head(heads + 1).astype(jnp.bfloat16)
+        length = keys.shape[0]
+        causal = lax.broadcasted_iota(jnp.int32, (length, length), 0) >= lax.broadcasted_iota(jnp.int32, (length, length), 1)
+        parts = []
+        for i in range(heads):
+            query = rotate(head(i), cos_tab, sin_tab).astype(jnp.bfloat16)
+            scores = lax.dot_general(query, keys, (((1,), (1,)), ((), ())), preferred_element_type=jnp.float32) * (size ** -0.5)
+            scores = jnp.where(causal, scores, MASK_VALUE)
+            weights = jnp.exp(scores - jnp.max(scores, axis=-1, keepdims=True))
+            weights = (weights / jnp.sum(weights, axis=-1, keepdims=True)).astype(jnp.bfloat16)
+            parts.append(jnp.dot(weights, vals, preferred_element_type=jnp.float32).astype(jnp.bfloat16))
+        return jnp.concatenate(parts, axis=-1)
+
     def st_pre(s):
         @pl.when(s == 0)
         def _():
             loads[0].wait()
-        left = lhs[s]
+        left = self_attention(s) if has_attn else lhs[s]
         for n in range(dim // TILE):
             cols = pl.ds(n * TILE, TILE)
             prod = jnp.dot(left, wv_pre[:, cols], preferred_element_type=jnp.float32)
@@ -234,12 +299,18 @@
             for ld in loads[len(loads) - n_post:]:
                 ld.wait()
         left = out[s].reshape(8 * rows, dim)
-        if swiglu:
+        if mode == 'swiglu':
             for n in range(res.shape[-1] // TILE):
                 cols = pl.ds(n * TILE, TILE)
                 gate_proj = jnp.dot(left, wv_post[0][:, cols], preferred_element_type=jnp.float32)
                 up_proj = jnp.dot(left, wv_post[1][:, cols], preferred_element_type=jnp.float32)
                 res[s, :, cols] = (jax.nn.silu(gate_proj) * up_proj).astype(jnp.bfloat16)
+        elif mode == 'queries':
+            length, size = left.shape[0], q_gain.shape[-1]
+            for n in range(wv_post[0].shape[-1] // size):
+                prod = jnp.dot(left, wv_post[0][:, pl.ds(n * size, size)], preferred_element_type=jnp.float32)
+                mean_sq = jnp.mean(prod * prod, axis=-1, keepdims=True)
+                res[s, n * length:(n + 1) * length] = (prod * lax.rsqrt(mean_sq + NORM_EPS) * f32(q_gain[0:1])).astype(jnp.bfloat16)
         else:
             base = 0
             for w in wv_post:
@@ -264,9 +335,16 @@
             @pl.when((s >= 0) & (s < samples))
             def _(stage=stage, s=s):
                 stage(s)
+        if chunks:
+            for action, lag in ((chunk_forward, 2), (chunk_send, 0)):
+                j = t - lag
+
+                @pl.when((j >= 0) & (j < chunks))
+                def _(action=action, j=j):
+                    action(j)
         return carry
 
-    lax.fori_loop(0, samples + len(stages) - 1, step, 0)
+    lax.fori_loop(0, max(samples + len(stages) - 1, chunks + 2), step, 0)
 
     def drain(s, carry):
         for flow in flows:
@@ -274,6 +352,18 @@
         return carry
 
     lax.fori_loop(0, samples, drain, 0)
+
+    def finish(j, carry):
+        for p in range(2):
+            for kind in range(2):
+                near_copy(p, kind, j).wait_send()
+        fwd_copy(0, j).wait()
+        return carry
+
+    if chunks:
+        lax.fori_loop(0, chunks, finish, 0)
+    if has_far:
+        far_copy.wait()
     for k in range(1, 8 if has_aux else 1):
         src = lax.rem(me + 8 - k, 8)
         pltpu.make_async_remote_copy(src_ref=aux, dst_ref=aux_out.at[src], send_sem=aux_send.at[k], recv_sem=aux_recv.at[k], device_id={'tp': pc}, device_id_type=MESH).wait_recv()
@@ -281,7 +371,7 @@
         cp.wait_send()
 
 
-def fused(cid, resid, lhs=None, w_pre=None, gate=None, gain=None, w_post=(), swiglu=False, aux=None):
+def fused(cid, resid, lhs=None, w_pre=None, gate=None, gain=None, w_post=(), mode=None, aux=None, rope=None, q_gain=None, gain_row=0, mine=None, near_part=None, far_src=None):
     samples, rows, dim = resid.shape
     bf16 = jnp.bfloat16
     half = dim // 2
@@ -307,29 +397,53 @@
             pltpu.VMEM((samples, 2, rows, half), bf16), pltpu.VMEM((samples, 2, rows, half), bf16),
             pltpu.VMEM((samples, 2, rows, half), bf16), pltpu.VMEM((samples, 2, rows, half), bf16),
             pltpu.VMEM((samples, rows, half), bf16), pltpu.VMEM((samples, rows, half), bf16)]
+    if rope is not None:
+        add(rope[0], vmem)
+        add(rope[1], vmem)
+    if q_gain is not None:
+        add(q_gain, vmem)
     add(resid, vmem)
     if gate is not None:
         add(gate, vmem)
     if has_post:
-        add(gain.reshape(1, dim), vmem)
+        add(gain, vmem)
         for w in w_post:
             add(w, hbm)
             flops += 2 * samples * 8 * rows * w.size
             scratch.append(pltpu.VMEM(w.shape, bf16))
-        if swiglu:
+        if mode == 'swiglu':
             outs.append(jax.ShapeDtypeStruct((samples, 8 * rows, w_post[0].shape[1]), bf16))
+        elif mode == 'queries':
+            size = q_gain.shape[1]
+            outs.append(jax.ShapeDtypeStruct((samples, 8 * rows * (w_post[0].shape[1] // size), size), bf16))
         else:
             outs.append(jax.ShapeDtypeStruct((samples, 8 * rows, sum(w.shape[1] for w in w_post)), jnp.float32))
         scratch.append(pltpu.VMEM((samples, 2, 2, 2, rows, dim), bf16))
     if aux is not None:
         add(aux, vmem)
         outs.append(jax.ShapeDtypeStruct((8,) + aux.shape, aux.dtype))
+    if near_part is not None:
+        add(mine[0], hbm)
+        add(mine[1], hbm)
+        part_shape = (2, mine[0].shape[0] // 4, mine[0].shape[1])
+    if far_src is not None:
+        add(far_src, hbm)
+    out_specs = [vmem] * len(outs)
+    if near_part is not None:
+        outs.append(jax.ShapeDtypeStruct((3,) + part_shape, bf16))
+    if far_src is not None:
+        outs.append(jax.ShapeDtypeStruct(far_src.shape, bf16))
+    out_specs += [hbm] * (len(outs) - len(out_specs))
     scratch += [pltpu.SemaphoreType.DMA((FLOWS, samples)), pltpu.SemaphoreType.DMA((FLOWS, samples)), pltpu.SemaphoreType.DMA((1 + len(w_post),))]
+    if near_part is not None:
+        scratch += [pltpu.SemaphoreType.DMA((2, 2, part_shape[1] // CHUNK))] * 2 + [pltpu.SemaphoreType.DMA((part_shape[1] // CHUNK,))] * 2
+    if far_src is not None:
+        scratch += [pltpu.SemaphoreType.DMA] * 2
     if aux is not None:
         scratch += [pltpu.SemaphoreType.DMA((8,)), pltpu.SemaphoreType.DMA((8,))]
     return pl.pallas_call(
-        functools.partial(fused_kernel, samples, has_pre, has_post, swiglu, gate is not None, aux is not None, len(w_post)),
-        out_shape=tuple(outs), in_specs=specs, out_specs=tuple([vmem] * len(outs)),
+        functools.partial(fused_kernel, samples, has_pre, has_post, mode, gate is not None, aux is not None, rope is not None, len(w_post), gain_row, near_part, far_src is not None),
+        out_shape=tuple(outs), in_specs=specs, out_specs=tuple(out_specs),
         scratch_shapes=scratch, name=f'fused_{cid}',
         cost_estimate=pl.CostEstimate(flops=flops + 2 * 10 ** 10, bytes_accessed=10 ** 7, transcendentals=0),
         compiler_params=pltpu.CompilerParams(collective_id=cid, has_side_effects=True, vmem_limit_bytes=67043328),
@@ -340,18 +454,41 @@
 STAT = 8
 
 
-def cross_kernel(samples, q_ref, k_hbm, v_hbm, vis_ref, ctx, q_all, k_vm, v_vm, ob_l, ob_h, rec_x1, rec_y1, two_l, two_h, rec_y2, rec_x2, send, recv, ksem):
+def cross_kernel(samples, n_w, q_ref, seen_ref, gain_ref, own_hbm, par_hbm, *refs):
+    w_hbm, refs = refs[:n_w], refs[n_w:]
+    ctx, q_all, w_vm, vis_vm, k_vm, v_vm, ob_l, ob_h, rec_x1, rec_y1, two_l, two_h, rec_y2, rec_x2, send, recv, wsem, vsem = refs
     me = lax.axis_index('tp')
+    z = lax.axis_index('dp')
     x = (me // 2) % 2
     y = me // 4
     px, py = me + 2 - 4 * x, me + 4 - 8 * y
     rows, size = q_ref.shape[1:]
+    vis_rows = own_hbm.shape[1]
     top, low = pl.ds(0, rows // 2), pl.ds(rows // 2, rows // 2)
     half = size // 2
     scale = size ** -0.5
-    loads = [pltpu.make_async_copy(k_hbm, k_vm, ksem.at[0]), pltpu.make_async_copy(v_hbm, v_vm, ksem.at[1])]
+    sources = [w_hbm[0], w_hbm[1]]
+    targets = [w_vm.at[0, :, pl.ds(0, size)], w_vm.at[0, :, pl.ds(size, size)]]
+    part = w_hbm[2].shape[2]
+    for i, ref in enumerate(w_hbm[2:]):
+        base = part * (2 * (i // 2) + (z + i) % 2)
+        for p in range(3):
+            for kind in range(2):
+                sources.append(ref.at[p, kind])
+                targets.append(w_vm.at[1 + p, pl.ds(base, part), pl.ds(kind * size, size)])
+    loads = [pltpu.make_async_copy(src, dst, wsem.at[i]) for i, (src, dst) in enumerate(zip(sources, targets))]
+
+    def vis_loads(s):
+        spot = s % 2
+        return [pltpu.make_async_copy(src.at[s], vis_vm.at[spot, i], vsem.at[spot, i]) for i, src in enumerate((own_hbm, par_hbm))]
+
+    for ld in vis_loads(0):
+        ld.start()
     for ld in loads:
         ld.start()
+
+    def near(ref, s, p):
+        return ref.at[s, (1 - y) if p // 2 else y, (1 - x) if p % 2 else x]
 
     def ends(flow, s):
         own, sx, sy, sd = q_all.at[s, y, x], q_all.at[s, y, 1 - x], q_all.at[s, 1 - y, x], q_all.at[s, 1 - y, 1 - x]
@@ -410,27 +547,22 @@
     def st_c(s):
         got(Q_YF, s)
         got(Q_XF, s)
-
-        @pl.when(s == 0)
-        def _():
-            for ld in loads:
-                ld.wait()
-        seen = vis_ref[s] > 0
+        seen = seen_ref[s] > 0
+        spot = s % 2
         for p in range(4):
             cols = pl.ds(p * size, size)
-            keys = k_vm[:, s, :, cols].reshape(-1, size)
-            vals = v_vm[:, s, :, cols].reshape(-1, size)
-            scores = lax.dot_general(keys, q_all[s, p // 2, p % 2], (((1,), (1,)), ((), ())), preferred_element_type=jnp.float32) * scale
+            keys = k_vm[spot, :, cols]
+            vals = v_vm[spot, :, cols]
+            scores = lax.dot_general(keys, near(q_all, s, p)[...], (((1,), (1,)), ((), ())), preferred_element_type=jnp.float32) * scale
             scores = jnp.where(seen, scores, MASK_VALUE)
             peak = jnp.max(scores, axis=0, keepdims=True)
             weights = jnp.exp(scores - peak)
             total = jnp.sum(weights, axis=0, keepdims=True)
             context = lax.dot_general(vals, weights.astype(jnp.bfloat16), (((0,), (0,)), ((), ())), preferred_element_type=jnp.float32)
             stats = stat_block(peak, total)
-            ob_l[s, p // 2, p % 2, :half] = context[:half]
-            ob_h[s, p // 2, p % 2, :half] = context[half:]
-            ob_l[s, p // 2, p % 2, half:] = stats
-            ob_h[s, p // 2, p % 2, half:] = stats
+            for ref, part in ((ob_l, context[:half]), (ob_h, context[half:])):
+                near(ref, s, p)[:half] = part
+                near(ref, s, p)[half:] = stats
         start(O_X1, s)
         start(O_Y1, s)
 
@@ -460,18 +592,44 @@
         for r in range(reps):
             ctx[s, :, r * size:(r + 1) * size] = whole[r * ctx.shape[1]:(r + 1) * ctx.shape[1]]
 
-    stages = [st_a, st_b, st_c, st_d, st_e]
+    def st_j(s):
+        @pl.when(s == 0)
+        def _():
+            for ld in loads:
+                ld.wait()
+
+        @pl.when(s + 1 < samples)
+        def _():
+            for ld in vis_loads(s + 1):
+                ld.start()
+        for ld in vis_loads(s):
+            ld.wait()
+        spot = s % 2
+        rows_in = vis_vm[spot].reshape(2 * vis_rows, -1)
+        for p in range(4):
+            cols = pl.ds(p * size, size)
+            keys = jnp.dot(rows_in, w_vm[p, :, pl.ds(0, size)], preferred_element_type=jnp.float32)
+            mean_sq = jnp.mean(keys * keys, axis=-1, keepdims=True)
+            k_vm[spot, :, cols] = (keys * lax.rsqrt(mean_sq + NORM_EPS) * gain_ref[1:2].astype(jnp.float32)).astype(jnp.bfloat16)
+            v_vm[spot, :, cols] = jnp.dot(rows_in, w_vm[p, :, pl.ds(size, size)], preferred_element_type=jnp.float32).astype(jnp.bfloat16)
+
+    stages = [(st_d, 2), (st_e, 3), (st_c, 1), (st_b, 0), (st_j, 0)]
 
     def step(t, carry):
-        for k, stage in enumerate(stages):
-            s = t - k
+        for stage, lag in stages:
+            s = t - lag
 
             @pl.when((s >= 0) & (s < samples))
             def _(stage=stage, s=s):
                 stage(s)
         return carry
 
-    lax.fori_loop(0, samples + len(stages) - 1, step, 0)
+    def first(s, carry):
+        st_a(s)
+        return carry
+
+    lax.fori_loop(0, samples, first, 0)
+    lax.fori_loop(0, samples + 3, step, 0)
 
     def drain(s, carry):
         for flow in range(8):
@@ -481,8 +639,9 @@
     lax.fori_loop(0, samples, drain, 0)
 
 
-def cross(cid, queries, keys, vals, seen, tokens):
+def cross(cid, queries, seen, gain, own, partner, weights, tokens):
     samples, rows, size = queries.shape
+    vis_rows, dim = own.shape[1:]
     f32, bf16 = jnp.float32, jnp.bfloat16
     half = size // 2
     vmem = pl.BlockSpec(memory_space=pltpu.VMEM)
@@ -490,45 +649,21 @@
     wide = pltpu.VMEM((samples, 2, half + STAT, rows), f32)
     one = pltpu.VMEM((samples, half + STAT, rows), f32)
     both = pltpu.VMEM((samples, 2, 2, half + STAT, rows), f32)
+    heads = pltpu.VMEM((2, 2 * vis_rows, 4 * size), bf16)
     return pl.pallas_call(
-        functools.partial(cross_kernel, samples),
+        functools.partial(cross_kernel, samples, len(weights)),
         out_shape=jax.ShapeDtypeStruct((samples, tokens, rows // tokens * size), bf16),
-        in_specs=[vmem, hbm, hbm, vmem], out_specs=vmem,
+        in_specs=[vmem, vmem, vmem] + [hbm] * (2 + len(weights)), out_specs=vmem,
         scratch_shapes=[
-            pltpu.VMEM((samples, 2, 2, rows, size), bf16), pltpu.VMEM(keys.shape, bf16), pltpu.VMEM(vals.shape, bf16),
+            pltpu.VMEM((samples, 2, 2, rows, size), bf16), pltpu.VMEM((4, dim, 2 * size), bf16),
+            pltpu.VMEM((2, 2, vis_rows, dim), bf16), heads, heads,
             both, both, wide, wide, wide, wide, one, one,
-            pltpu.SemaphoreType.DMA((8, samples)), pltpu.SemaphoreType.DMA((8, samples)), pltpu.SemaphoreType.DMA((2,))],
+            pltpu.SemaphoreType.DMA((8, samples)), pltpu.SemaphoreType.DMA((8, samples)),
+            pltpu.SemaphoreType.DMA((26,)), pltpu.SemaphoreType.DMA((2, 2))],
         name=f'cross_{cid}',
-        cost_estimate=pl.CostEstimate(flops=5 * 10 ** 10, bytes_accessed=10 ** 7, transcendentals=0),
+        cost_estimate=pl.CostEstimate(flops=8 * 10 ** 10, bytes_accessed=10 ** 7, transcendentals=0),
         compiler_params=pltpu.CompilerParams(collective_id=cid, has_side_effects=True, vmem_limit_bytes=60 * 2 ** 20),
-    )(queries, keys, vals, seen)
-
-
-def kv_kernel(head_dim, own_ref, par_ref, wk_ref, wv_ref, gain_ref, k_ref, v_ref):
-    for i, src in enumerate((own_ref, par_ref)):
-        rows = src[0]
-        for n in range(wk_ref.shape[1] // head_dim):
-            cols = pl.ds(n * head_dim, head_dim)
-            keys = jnp.dot(rows, wk_ref[:, cols], preferred_element_type=jnp.float32)
-            mean_sq = jnp.mean(keys * keys, axis=-1, keepdims=True)
-            k_ref[i, 0, :, cols] = (keys * lax.rsqrt(mean_sq + NORM_EPS) * gain_ref[...].astype(jnp.float32)).astype(jnp.bfloat16)
-            v_ref[i, 0, :, cols] = jnp.dot(rows, wv_ref[:, cols], preferred_element_type=jnp.float32).astype(jnp.bfloat16)
-
-
-def project_kv(own, partner, wk, wv, gain):
-    samples, rows, dim = own.shape
-    width = wk.shape[1]
-    rows_spec = pl.BlockSpec((1, rows, dim), lambda s: (s, 0, 0))
-    weight_spec = pl.BlockSpec((dim, width), lambda s: (0, 0))
-    out_spec = pl.BlockSpec((2, 1, rows, width), lambda s: (0, s, 0, 0))
-    out = jax.ShapeDtypeStruct((2, samples, rows, width), jnp.bfloat16)
-    return pl.pallas_call(
-        functools.partial(kv_kernel, gain.shape[0]), grid=(samples,),
-        in_specs=[rows_spec, rows_spec, weight_spec, weight_spec, pl.BlockSpec((1, gain.shape[0]), lambda s: (0, 0))],
-        out_specs=(out_spec, out_spec), out_shape=(out, out), name='project_kv',
-        cost_estimate=pl.CostEstimate(flops=8 * samples * rows * dim * width, bytes_accessed=10 ** 8, transcendentals=0),
-        compiler_params=pltpu.CompilerParams(vmem_limit_bytes=60 * 2 ** 20),
-    )(own, partner, wk, wv, gain.reshape(1, -1))
+    )(queries, seen, gain, own, partner, *weights)
 
 
 def solution(mesh):
@@ -548,36 +683,27 @@
         kv_local = wk_a.shape[1] // head_dim
         rep_heads = wq_a.shape[1] // head_dim // kv_local
 
-        same_core = [[core + 2 * chip for chip in range(4)] for core in range(2)]
-        wk_all = lax.all_gather(wk_b, 'tp', axis=1, tiled=True, axis_index_groups=same_core)
-        wv_all = lax.all_gather(wv_b, 'tp', axis=1, tiled=True, axis_index_groups=same_core)
+        gains = jnp.stack([ln1_a, ln2_a, ln1_b, ln2_b])
+        head_gains = jnp.stack([q_norm, k_norm])
         vis_partner = lax.ppermute(vision, 'tp', [(i, i ^ 1) for i in range(8)])
 
         small = jnp.concatenate([positions.reshape(-1), tile_mask.reshape(-1)])
         aux = jnp.pad(small, (0, 1024 - small.shape[0])).reshape(8, 128)
-        proj, aux_all = fused(1, hidden, gain=ln1_a, w_post=(wq_a, wk_a, wv_a), aux=aux)
+        proj, aux_all, near_one = fused(1, hidden, gain=gains, gain_row=0, w_post=(wq_a, wk_a, wv_a), aux=aux, mine=(wk_b, wv_b), near_part=0)
         aux_all = aux_all.reshape(8, 1024)
         pos_all = aux_all[:, :samples * rows].reshape(8, samples, rows).transpose(1, 0, 2).reshape(samples, tokens)
         mask_all = aux_all[:, samples * rows:samples * rows * (1 + tiles)].reshape(8, samples, rows, tiles).transpose(1, 0, 2, 3).reshape(samples, tokens, tiles)
 
         angles = pos_all.astype(jnp.float32)[..., None] * rope_table(head_dim)
-        cos_tab = jnp.cos(angles)[:, :, None, :]
-        sin_tab = jnp.sin(angles)[:, :, None, :]
-        proj = proj.reshape(samples, tokens, rep_heads + 2, head_dim)
-        rotated = rotate(proj[:, :, :rep_heads + 1], cos_tab, sin_tab).astype(jnp.bfloat16)
-        queries = rotated[:, :, :rep_heads].transpose(0, 2, 1, 3)[:, None]
-        context = self_attend(queries, rotated[:, :, rep_heads:], proj[:, :, rep_heads + 1:].astype(jnp.bfloat16))
-        context = context[:, 0].transpose(0, 2, 1, 3).reshape(samples, tokens, rep_heads * head_dim)
-        h_one, act = fused(2, hidden, lhs=context, w_pre=wo_a, gain=ln2_a, w_post=(wg_a, wu_a), swiglu=True)
-        h_two, queries = fused(3, h_one, lhs=act, w_pre=wd_a, gain=ln1_b, w_post=(wq_b,))
-        queries = rms_scale(queries.reshape(samples, tokens, rep_heads, head_dim), q_norm).astype(jnp.bfloat16)
-        queries = queries.transpose(0, 2, 1, 3).reshape(samples, rep_heads * tokens, head_dim)
-        keys, vals = project_kv(vision, vis_partner, wk_all, wv_all, k_norm)
+        rope = (jnp.cos(angles), jnp.sin(angles))
+        h_one, act, near_two, far_one = fused(2, hidden, lhs=proj, w_pre=wo_a, rope=rope, gain=gains, gain_row=1, w_post=(wg_a, wu_a), mode='swiglu', mine=(wk_b, wv_b), near_part=1, far_src=near_one)
+        h_two, queries, far_two = fused(3, h_one, lhs=act, w_pre=wd_a, gain=gains, gain_row=2, w_post=(wq_b,), mode='queries', q_gain=head_gains, far_src=near_two)
+        weights = (wk_b, wv_b, near_one, far_one, near_two, far_two)
         seen = jnp.tile(lax.dynamic_index_in_dim(mask_all, me // 2, axis=2, keepdims=False)[:, None, :], (1, 1, rep_heads))
-        context = cross(6, queries, keys, vals, seen, tokens)
+        context = cross(6, queries, seen, head_gains, vision, vis_partner, weights, tokens)
         row_keep = jnp.any(tile_mask > 0, axis=-1, keepdims=True).astype(jnp.float32)
         gate_vals = jnp.tanh(xgates.astype(jnp.float32))
-        h_three, act = fused(4, h_two, lhs=context, w_pre=wo_b, gate=gate_vals[0] * row_keep, gain=ln2_b, w_post=(wg_b, wu_b), swiglu=True)
+        h_three, act = fused(4, h_two, lhs=context, w_pre=wo_b, gate=gate_vals[0] * row_keep, gain=gains, gain_row=3, w_post=(wg_b, wu_b), mode='swiglu')
         return fused(5, h_three, lhs=act, w_pre=wd_b, gate=gate_vals[1] * row_keep)[0]
 
     return jax.shard_map(body, mesh=mesh, in_specs=in_specs, out_specs=act_spec, check_vma=False)

time: 530 us -> 439 us (0.83)
  Pallas kernels: 488 us -> 416 us
  between operations: 13.8 us -> 0.13 us
  local copies, waits for them, and re-layouts: 20.4 us -> 14.3 us
    pallas_call x2 -> x1, Pallas kernels: 140 us -> 89.9 us  [cross(): pl.pallas_call(functools.partial(cross_kernel, samples, len(weights)), ou...]
    pallas_call x5, Pallas kernels: 348 us -> 327 us  [fused(): pl.pallas_call(functools.partial(fused_kernel, samples, has_pre, has_post...]
    reshape x8 -> x0, local copies, waits for them, and re-layouts: 9.61 us -> none  [the longest x1 3.42 us: body(): proj = proj.reshape(samples, tokens, rep_heads + 2, head_dim)]
  transfers between devices with their start and end apart: 3 -> 1, of which waited for: 0 -> 0; matrix products, arithmetic and copies ran while one was open for 4% -> 4% of each run, Pallas kernels for 46% -> 51%
where the time goes in v2:
time: 439 us; the launch traced here: 438 us
  Pallas kernels  416 us (95%)
  local copies, waits for them, and re-layouts  14.3 us (3%)
  other arithmetic  6.39 us (1%)
    pallas_call x5, Pallas kernels, fused(): pl.pallas_call(functools.partial(fused_kernel, samples, has_pre, has_post...  327 us
    pallas_call x1, Pallas kernels, cross(): pl.pallas_call(functools.partial(cross_kernel, samples, len(weights)), ou...  89.9 us
  transfers between devices with their start and end apart: 1, of which 0 were waited for; matrix products, arithmetic and copies ran while one was open for 4% of the time, Pallas kernels for 51%

profile of v2, /device:TPU:0, one launch (start us, length us, event | category | flops | bytes accessed | tf_op | source)
XLA Modules:
  0.0 437.8 jit_solution(2776671896334262856)
XLA Ops:
  0.0 0.5 collective-permute-start
  0.5 0.7 stack.24
  1.2 0.7 stack.25
  1.9 0.7 stack.26
  2.7 0.7 stack.27
  3.4 0.8 copy.35
  4.2 0.1 reshape.58
  4.3 0.8 reshape.57
  5.1 0.1 pad_add_fusion
  5.1 0.6 pad_bitcast_fusion.refs_5_
  5.7 0.7 pad_maximum_fusion.refs_1_.refs_5_.refs_4_
  6.4 64.0 %fused_1.1 = (f32[6,128,1024]{2,1,0:T(8,128)}, s32[8,8,128]{2,1,0:T(8,128)}, bf16[3,2,896,256]{3,2,1,0:T(8,128)(2,1)}) custom-call(bf16[6,16,3584]{2,1,0:T(8,128)(2,1)} %refs_4_.3, bf16[4,3584]{1,0:T(4,128)(2,1)} %pad_maximum_fusion.refs_1_.refs_5_.refs_4_, bf16[3584,512]{1,0:T(8,128)(2,1)} %refs_2_.1, bf16[3584,256]{1,0:T(8,128)(2,1)} %refs_3_.1, ...), custom_call_target="tpu_custom_call" | custom-call | flops 25637144576 | bytes 10000000 | tf_op jit(solution)/shard_map/fused_1/pallas_call | solution.py:444
  70.4 0.8 copy.46
  71.2 0.1 slice.17
  71.3 0.1 copy.42
  71.4 0.1 copy.38
  71.5 0.1 reshape.62
  71.7 0.6 copy.47
  72.3 0.1 convert_element_type.18
  72.3 0.1 convert_element_type.20
  72.4 0.7 stack.29
  73.1 0.7 stack.30
  73.7 0.7 tanh.3
  74.4 0.6 fusion
  75.0 0.7 compare_reduce_fusion
  75.7 1.3 select_bitcast_fusion
  77.0 0.7 copy.39.refs_3_
  77.7 0.7 copy.40.refs_3_
  78.4 0.5 pad_maximum_fusion.1.refs_2_.gain_ref
  79.0 3.1 multiply_sine_fusion
  82.1 92.4 %fused_2.1 = (bf16[6,16,3584]{2,1,0:T(8,128)(2,1)}, bf16[6,128,1792]{2,1,0:T(8,128)(2,1)}, bf16[3,2,896,256]{3,2,1,0:T(8,128)(2,1)}, bf16[3,2,896,256]{3,2,1,0:T(8,128)(2,1)}) custom-call(f32[6,128,1024]{2,1,0:T(8,128)} %get-tuple-element.17.refs_0_, bf16[512,3584]{1,0:T(8,128)(2,1)} %refs_1_.5, f32[6,128,128]{2,1,0:T(8,128)} %get-tuple-element.30.refs_2_, ...), custom_call_target="tpu_custom_call" | custom-call | flops 42548576256 | bytes 10000000 | tf_op jit(solution)/shard_map/fused_2/pallas_call | solution.py:444
  174.5 66.7 %fused_3.1 = (bf16[6,16,3584]{2,1,0:T(8,128)(2,1)}, bf16[6,256,256]{2,1,0:T(8,128)(2,1)}, bf16[3,2,896,256]{3,2,1,0:T(8,128)(2,1)}) custom-call(bf16[6,128,1792]{2,1,0:T(8,128)(2,1)} %get-tuple-element.20.refs_0_, bf16[1792,3584]{1,0:T(8,128)(2,1)} %refs_1_.6, bf16[2,256]{1,0:T(2,128)(2,1)} %pad_maximum_fusion.1.refs_2_.gain_ref, ...), custom_call_target="tpu_custom_call" | custom-call | flops 32683575296 | bytes 10000000 | tf_op jit(solution)/shard_map/fused_3/pallas_call | solution.py:444
  241.2 0.0 collective-permute-done.par_hbm
  241.2 1.3 tile.11
  242.4 89.9 %cross_6.1.refs_0_ = bf16[6,128,512]{2,1,0:T(8,128)(2,1)} custom-call(bf16[6,256,256]{2,1,0:T(8,128)(2,1)} %get-tuple-element.23.q_ref, s32[6,1,256]{2,1,0:T(1,128)} %bitcast.30, bf16[2,256]{1,0:T(2,128)(2,1)} %pad_maximum_fusion.1.refs_2_.gain_ref, bf16[6,256,3584]{2,1,0:T(8,128)(2,1)} %own_hbm.1, bf16[6,256,3584]{2,1,0:T(8,128)(2,1)} %collective-permute-done.par_hbm, ...), custom_call_target="tpu_custom_call" | custom-call | flops 80000000000 | bytes 10000000 | tf_op jit(solution)/shard_map/cross_6/pallas_call | solution.py:653
  332.3 65.1 %fused_4.1 = (bf16[6,16,3584]{2,1,0:T(8,128)(2,1)}, bf16[6,128,1792]{2,1,0:T(8,128)(2,1)}) custom-call(bf16[6,128,512]{2,1,0:T(8,128)(2,1)} %cross_6.1.refs_0_, bf16[512,3584]{1,0:T(8,128)(2,1)} %refs_1_.8, bf16[6,16,3584]{2,1,0:T(8,128)(2,1)} %get-tuple-element.26.refs_2_, f32[6,16,1]{2,1,0:T(8,128)} %copy.39.refs_3_, ...), custom_call_target="tpu_custom_call" | custom-call | flops 42548576256 | bytes 10000000 | tf_op jit(solution)/shard_map/fused_4/pallas_call | solution.py:444
  397.5 38.4 %fused_5.1 = bf16[6,16,3584]{2,1,0:T(8,128)(2,1)} custom-call(bf16[6,128,1792]{2,1,0:T(8,128)(2,1)} %get-tuple-element.27.refs_0_, bf16[1792,3584]{1,0:T(8,128)(2,1)} %refs_1_.9, bf16[6,16,3584]{2,1,0:T(8,128)(2,1)} %get-tuple-element.28.refs_2_, f32[6,16,1]{2,1,0:T(8,128)} %copy.40.refs_3_), custom_call_target="tpu_custom_call" | custom-call | flops 29865003008 | bytes 10000000 | tf_op jit(solution)/shard_map/fused_5/pallas_call | solution.py:444
  435.8 2.0 copy.49
  (3 shorter events, 0.0 us)
Async XLA Ops:
  0.0 241.2 %collective-permute-start = (bf16[6,256,3584]{2,1,0:T(8,128)(2,1)}, bf16[6,256,3584]{2,1,0:T(8,128)(2,1)}, u32[]{:S(2)}, u32[]{:S(2)}) collective-permute-start(bf16[6,256,3584]{2,1,0:T(8,128)(2,1)} %own_hbm.1), channel_id=1, source_target_pairs={{0,1},{1,0},{2,3},{3,2},{4,5},{5,4},{6,7},{7,6},{8,9},{9,8},{10,11... | collective-permute-start | bytes 33030152 | tf_op jit(solution)/shard_map/ppermute | solution.py:688

commit v3 on v2

--- a/solution.py
+++ b/solution.py
@@ -33,12 +33,6 @@
     return jnp.array(freq_list, dtype=jnp.float32)
 
 
-def rms_scale(values, norm_gain):
-    values = values.astype(jnp.float32)
-    mean_sq = jnp.mean(values * values, axis=-1, keepdims=True)
-    return values * lax.rsqrt(mean_sq + NORM_EPS) * norm_gain.astype(jnp.float32)
-
-
 def rotate(values, cos_tab, sin_tab):
     half_dim = values.shape[-1] // 2
     first_half = values[..., :half_dim]
@@ -46,58 +40,50 @@
     return jnp.concatenate([first_half * cos_tab - second_half * sin_tab, second_half * cos_tab + first_half * sin_tab], axis=-1)
 
 
-def self_attend(queries, key_vecs, val_vecs):
-    seq_len = queries.shape[3]
-    head_dim = queries.shape[4]
-    scores = jnp.einsum('bgrtd,bsgd->bgrts', queries, key_vecs, preferred_element_type=jnp.float32) * (head_dim ** -0.5)
-    causal = lax.broadcasted_iota(jnp.int32, (seq_len, seq_len), 0) >= lax.broadcasted_iota(jnp.int32, (seq_len, seq_len), 1)
-    weights = jax.nn.softmax(jnp.where(causal, scores, MASK_VALUE), axis=-1).astype(jnp.bfloat16)
-    return jnp.einsum('bgrts,bsgd->bgrtd', weights, val_vecs, preferred_element_type=jnp.float32).astype(jnp.bfloat16)
-
-
-def cross_attend(queries, key_vecs, val_vecs, visible):
-    batch_len, kv_groups, rep_heads, seq_len, head_dim = queries.shape
-    vis_len = key_vecs.shape[1]
-    tile_count = visible.shape[2]
-    scores = jnp.einsum('bgrtd,bsgd->bgrts', queries, key_vecs, preferred_element_type=jnp.float32) * (head_dim ** -0.5)
-    scores = scores.reshape(batch_len, kv_groups, rep_heads, seq_len, tile_count, vis_len // tile_count)
-    scores = jnp.where(visible[:, None, None, :, :, None], scores, MASK_VALUE)
-    weights = jax.nn.softmax(scores.reshape(batch_len, kv_groups, rep_heads, seq_len, vis_len), axis=-1).astype(jnp.bfloat16)
-    return jnp.einsum('bgrts,bsgd->bgrtd', weights, val_vecs, preferred_element_type=jnp.float32).astype(jnp.bfloat16)
-
-
 MESH = pl.DeviceIdType.MESH
 D_SUM, X_ONE, Y_ONE, Y_TWO, X_TWO, X_OWN, Y_OWN, C_OWN, Y_FWD, X_FWD, C_X, C_Y, C_DIAG = range(13)
 FLOWS = 13
 TILE = 256
-CHUNK = 112
-
-
-def fused_kernel(samples, has_pre, has_post, mode, gated, has_aux, has_attn, n_post, gain_row, near_part, has_far, *refs):
+PLANE = (2, 2)
+CUBE = (2, 2, 2)
+CHUNKS = (112, 112)
+CHUNK_PAUSE = ((8, 0), (3, 4))
+
+
+def given(value):
+    return value is not None
+
+
+def fused_kernel(samples, has_pre, has_post, mode, gate_row, has_aux, has_attn, n_post, gain_row, near_part, has_far, has_kv, *refs):
     refs = list(refs)
-    take = lambda n: [refs.pop(0) for _ in range(n)]
-    lhs, w_pre = take(2) if has_pre else (None, None)
-    cos, sin = take(2) if has_attn else (None, None)
-    q_gain, = take(1) if mode == 'queries' else (None,)
-    resid, = take(1)
-    gate, = take(1) if gated else (None,)
-    gain, = take(1) if has_post else (None,)
+    one = lambda held: refs.pop(0) if held else None
+    take = lambda n, held=True: [one(held) for _ in range(n)]
+    lhs, w_pre = take(2, has_pre)
+    cos, sin = take(2, has_attn)
+    q_gain = one(mode == 'queries')
+    vis_src, kv_w = take(2, has_kv), take(2, has_kv)
+    resid = one(True)
+    tile_mask, xgates = take(2, given(gate_row))
+    gain = one(has_post)
     w_post = take(n_post)
-    aux, = take(1) if has_aux else (None,)
-    own_w = take(2) if near_part is not None else None
-    far_src, = take(1) if has_far else (None,)
-    h_out, = take(1) if has_pre else (None,)
-    res, = take(1) if has_post else (None,)
-    aux_out, = take(1) if has_aux else (None,)
-    near_out, = take(1) if near_part is not None else (None,)
-    far_out, = take(1) if has_far else (None,)
+    aux = one(has_aux)
+    own_w = take(2, given(near_part))
+    far_src = one(has_far)
+    h_out = one(has_pre)
+    res = one(has_post)
+    aux_out = one(has_aux)
+    kv_out = one(has_kv)
+    near_out = one(given(near_part))
+    far_out = one(has_far)
     if has_pre:
         wv_pre, part, rec_d, acc, rec_x1, rec_y1, two_l, two_h, rec_y2, rec_x2 = take(10)
     wv_post = take(n_post)
-    out, = take(1) if has_post else (None,)
+    out = one(has_post)
+    gate = one(given(gate_row))
+    vis_vm, kv_vm, vis_sem, kv_sem = take(4, has_kv)
     send, recv, wsem = take(3)
-    near_send, near_recv, fwd_send, fwd_recv = take(4) if near_part is not None else (None,) * 4
-    far_send, far_recv = take(2) if has_far else (None, None)
+    near_send, near_recv, fwd_send, fwd_recv = take(4, given(near_part))
+    far_send, far_recv = take(2, has_far)
     me = lax.axis_index('tp')
     c = me % 2
     x = (me // 2) % 2
@@ -111,11 +97,40 @@
 
     loads = []
     if has_pre:
-        loads.append(pltpu.make_async_copy(w_pre, wv_pre, wsem.at[0]))
+        for i, span in enumerate((lo, hi)):
+            loads.append(pltpu.make_async_copy(w_pre.at[:, span], wv_pre.at[:, span], wsem.at[i]))
     for i in range(n_post):
-        loads.append(pltpu.make_async_copy(w_post[i], wv_post[i], wsem.at[1 + i]))
+        loads.append(pltpu.make_async_copy(w_post[i], wv_post[i], wsem.at[2 + i]))
     for ld in loads:
         ld.start()
+
+    def vis_loads(s):
+        return [pltpu.make_async_copy(src.at[s], vis_vm.at[s % 2, i], vis_sem.at[s % 2, i]) for i, src in enumerate(vis_src)]
+
+    kv_loads = []
+    if has_kv:
+        size = kv_w[0].shape[1]
+        kv_loads = [pltpu.make_async_copy(src, kv_vm.at[:, pl.ds(i * size, size)], kv_sem.at[i]) for i, src in enumerate(kv_w)]
+        for ld in kv_loads + vis_loads(0):
+            ld.start()
+
+    def st_kv(s):
+        @pl.when(s == 0)
+        def _():
+            for ld in kv_loads:
+                ld.wait()
+
+        @pl.when(s + 1 < samples)
+        def _():
+            for ld in vis_loads(s + 1):
+                ld.start()
+        for ld in vis_loads(s):
+            ld.wait()
+        rows_in = vis_vm[s % 2].reshape(-1, dim)
+        keys = jnp.dot(rows_in, kv_vm[:, pl.ds(0, size)], preferred_element_type=jnp.float32)
+        mean_sq = jnp.mean(keys * keys, axis=-1, keepdims=True)
+        kv_out[s, :, pl.ds(0, size)] = (keys * lax.rsqrt(mean_sq + NORM_EPS) * f32(q_gain[1:2])).astype(jnp.bfloat16)
+        kv_out[s, :, pl.ds(size, size)] = jnp.dot(rows_in, kv_vm[:, pl.ds(size, size)], preferred_element_type=jnp.float32).astype(jnp.bfloat16)
 
     def slot(s, dy, dx, dc):
         return out.at[s, (1 - y) if dy else y, (1 - x) if dx else x, (1 - c) if dc else c]
@@ -165,6 +180,10 @@
         mean_sq = jnp.mean(values * values, axis=-1, keepdims=True)
         return (values * lax.rsqrt(mean_sq + NORM_EPS) * f32(gain[gain_row:gain_row + 1])).astype(jnp.bfloat16)
 
+    if given(gate_row):
+        keep = jnp.where(jnp.max(tile_mask[...], axis=-1, keepdims=True) > 0, 1.0, 0.0)
+        gate[...] = jnp.tanh(jnp.full(keep.shape, xgates[gate_row], jnp.float32)) * keep
+
     barrier = pltpu.get_barrier_semaphore()
     peers = [lax.rem(me + k, 8) for k in range(1, 8)] if has_aux else [pc, px, py]
     for who in peers:
@@ -173,15 +192,16 @@
         pl.semaphore_signal(barrier, inc=1, device_id={'dp': pz}, device_id_type=MESH)
     pl.semaphore_wait(barrier, len(peers) + (1 if has_far else 0))
 
-    part_rows = near_out.shape[2] if near_part is not None else 0
-    chunks = part_rows // CHUNK
+    chunk = CHUNKS[near_part or 0]
+    part_rows = near_out.shape[2] if given(near_part) else 0
+    chunks = part_rows // chunk
 
     def near_copy(p, kind, j):
-        first = part_rows * (2 * near_part + z % 2) + j * CHUNK
-        return pltpu.make_async_remote_copy(src_ref=own_w[kind].at[pl.ds(pl.multiple_of(first, CHUNK), CHUNK)], dst_ref=near_out.at[p, kind, pl.ds(j * CHUNK, CHUNK)], send_sem=near_send.at[p, kind, j], recv_sem=near_recv.at[p, kind, j], device_id={'tp': (px, py)[p]}, device_id_type=MESH)
+        first = part_rows * (2 * near_part + z % 2) + j * chunk
+        return pltpu.make_async_remote_copy(src_ref=own_w[kind].at[pl.ds(pl.multiple_of(first, chunk), chunk)], dst_ref=near_out.at[p, kind, pl.ds(j * chunk, chunk)], send_sem=near_send.at[p, kind, j], recv_sem=near_recv.at[p, kind, j], device_id={'tp': (px, py)[p]}, device_id_type=MESH)
 
     def fwd_copy(p, j):
-        span = pl.ds(j * CHUNK, CHUNK)
+        span = pl.ds(j * chunk, chunk)
         return pltpu.make_async_remote_copy(src_ref=near_out.at[p, :, span], dst_ref=near_out.at[2, :, span], send_sem=fwd_send.at[j], recv_sem=fwd_recv.at[j], device_id={'tp': (py, px)[p]}, device_id_type=MESH)
 
     def chunk_send(j):
@@ -235,11 +255,12 @@
         return jnp.concatenate(parts, axis=-1)
 
     def st_pre(s):
-        @pl.when(s == 0)
-        def _():
-            loads[0].wait()
         left = self_attention(s) if has_attn else lhs[s]
         for n in range(dim // TILE):
+            if n * TILE % half == 0:
+                @pl.when(s == 0)
+                def _(n=n):
+                    loads[n * TILE // half].wait()
             cols = pl.ds(n * TILE, TILE)
             prod = jnp.dot(left, wv_pre[:, cols], preferred_element_type=jnp.float32)
             part[s, :, :, :, :, cols] = prod.astype(jnp.bfloat16).reshape(2, 2, 2, rows, TILE)
@@ -263,7 +284,7 @@
         got(Y_TWO, s)
         got(X_TWO, s)
         total = jnp.concatenate([f32(two_l[s, y]) + f32(rec_y2[s]), f32(two_h[s, x]) + f32(rec_x2[s])], axis=-1)
-        if gated:
+        if given(gate_row):
             total = total * gate[s]
         new = (f32(resid[s]) + total).astype(jnp.bfloat16)
         h_out[s] = new
@@ -310,7 +331,7 @@
             for n in range(wv_post[0].shape[-1] // size):
                 prod = jnp.dot(left, wv_post[0][:, pl.ds(n * size, size)], preferred_element_type=jnp.float32)
                 mean_sq = jnp.mean(prod * prod, axis=-1, keepdims=True)
-                res[s, n * length:(n + 1) * length] = (prod * lax.rsqrt(mean_sq + NORM_EPS) * f32(q_gain[0:1])).astype(jnp.bfloat16)
+                res[s, n * length:(n + 1) * length] = (prod * lax.rsqrt(mean_sq + NORM_EPS) * f32(q_gain[0:1]) * (size ** -0.5)).astype(jnp.bfloat16)
         else:
             base = 0
             for w in wv_post:
@@ -319,32 +340,37 @@
                     base += TILE
 
     flows, stages = [], []
+    late = 3 if has_pre else 0
     if has_pre:
-        stages += [st_pre, st_r1, st_r2, st_r3]
+        stages += [(st_pre, 0), (st_r1, 1), (st_r2, 2), (st_r3, 3)]
         flows += [D_SUM, X_ONE, Y_ONE, Y_TWO, X_TWO]
     else:
-        stages += [st_g1]
+        stages += [(st_g1, 0)]
     if has_post:
-        stages += [st_g2, st_g3, st_g4]
+        stages += [(st_g2, late + 1), (st_g3, late + 2), (st_g4, late + 3)]
         flows += [X_OWN, Y_OWN, C_OWN, Y_FWD, X_FWD, C_X, C_Y, C_DIAG]
+    if has_kv:
+        stages += [(st_kv, late + 3)]
+    steps = samples + max(lag for _, lag in stages)
 
     def step(t, carry):
-        for k, stage in enumerate(stages):
-            s = t - k
+        for stage, lag in stages:
+            s = t - lag
 
             @pl.when((s >= 0) & (s < samples))
             def _(stage=stage, s=s):
                 stage(s)
         if chunks:
             for action, lag in ((chunk_forward, 2), (chunk_send, 0)):
-                j = t - lag
-
-                @pl.when((j >= 0) & (j < chunks))
-                def _(action=action, j=j):
-                    action(j)
+                early, pause = CHUNK_PAUSE[near_part]
+                u = t - lag
+                for begin, end, off in ((0, early, 0), (early + pause, chunks + pause, pause)):
+                    @pl.when((u >= begin) & (u < end))
+                    def _(action=action, j=u - off):
+                        action(j)
         return carry
 
-    lax.fori_loop(0, max(samples + len(stages) - 1, chunks + 2), step, 0)
+    lax.fori_loop(0, max(steps, chunks + 2 + CHUNK_PAUSE[near_part][1]) if chunks else steps, step, 0)
 
     def drain(s, carry):
         for flow in flows:
@@ -371,11 +397,11 @@
         cp.wait_send()
 
 
-def fused(cid, resid, lhs=None, w_pre=None, gate=None, gain=None, w_post=(), mode=None, aux=None, rope=None, q_gain=None, gain_row=0, mine=None, near_part=None, far_src=None):
+def fused(cid, resid, lhs=None, w_pre=None, gate=None, gain=None, w_post=(), mode=None, aux=None, rope=None, q_gain=None, gain_row=0, mine=None, near_part=None, far_src=None, kv=None):
     samples, rows, dim = resid.shape
     bf16 = jnp.bfloat16
     half = dim // 2
-    has_pre, has_post = lhs is not None, gain is not None
+    has_pre, has_post = given(lhs), given(gain)
     vmem = pl.BlockSpec(memory_space=pltpu.VMEM)
     hbm = pl.BlockSpec(memory_space=pl.ANY)
     args, specs, outs, scratch = [], [], [], []
@@ -392,19 +418,22 @@
         outs.append(jax.ShapeDtypeStruct(resid.shape, bf16))
         scratch += [
             pltpu.VMEM(w_pre.shape, bf16),
-            pltpu.VMEM((samples, 2, 2, 2, rows, dim), bf16),
-            pltpu.VMEM((samples, 2, 2, rows, dim), bf16), pltpu.VMEM((samples, 2, 2, rows, dim), bf16),
-            pltpu.VMEM((samples, 2, rows, half), bf16), pltpu.VMEM((samples, 2, rows, half), bf16),
-            pltpu.VMEM((samples, 2, rows, half), bf16), pltpu.VMEM((samples, 2, rows, half), bf16),
-            pltpu.VMEM((samples, rows, half), bf16), pltpu.VMEM((samples, rows, half), bf16)]
-    if rope is not None:
+            pltpu.VMEM((samples, *CUBE, rows, dim), bf16),
+            pltpu.VMEM((samples, *PLANE, rows, dim), bf16), pltpu.VMEM((samples, *PLANE, rows, dim), bf16),
+            *[pltpu.VMEM((samples, 2, rows, half), bf16)] * 4,
+            *[pltpu.VMEM((samples, rows, half), bf16)] * 2]
+    if given(rope):
         add(rope[0], vmem)
         add(rope[1], vmem)
-    if q_gain is not None:
+    if given(q_gain):
         add(q_gain, vmem)
+    if given(kv):
+        for value in kv:
+            add(value, hbm)
     add(resid, vmem)
-    if gate is not None:
-        add(gate, vmem)
+    if given(gate):
+        add(gate[0], vmem)
+        add(gate[1], pl.BlockSpec(memory_space=pltpu.SMEM))
     if has_post:
         add(gain, vmem)
         for w in w_post:
@@ -418,31 +447,37 @@
             outs.append(jax.ShapeDtypeStruct((samples, 8 * rows * (w_post[0].shape[1] // size), size), bf16))
         else:
             outs.append(jax.ShapeDtypeStruct((samples, 8 * rows, sum(w.shape[1] for w in w_post)), jnp.float32))
-        scratch.append(pltpu.VMEM((samples, 2, 2, 2, rows, dim), bf16))
-    if aux is not None:
+        scratch.append(pltpu.VMEM((samples, *CUBE, rows, dim), bf16))
+    if given(aux):
         add(aux, vmem)
         outs.append(jax.ShapeDtypeStruct((8,) + aux.shape, aux.dtype))
-    if near_part is not None:
+    if given(kv):
+        outs.append(jax.ShapeDtypeStruct((samples, 2 * kv[0].shape[1], 2 * kv[2].shape[1]), bf16))
+    if given(near_part):
         add(mine[0], hbm)
         add(mine[1], hbm)
         part_shape = (2, mine[0].shape[0] // 4, mine[0].shape[1])
-    if far_src is not None:
+    if given(far_src):
         add(far_src, hbm)
     out_specs = [vmem] * len(outs)
-    if near_part is not None:
+    if given(near_part):
         outs.append(jax.ShapeDtypeStruct((3,) + part_shape, bf16))
-    if far_src is not None:
+    if given(far_src):
         outs.append(jax.ShapeDtypeStruct(far_src.shape, bf16))
     out_specs += [hbm] * (len(outs) - len(out_specs))
-    scratch += [pltpu.SemaphoreType.DMA((FLOWS, samples)), pltpu.SemaphoreType.DMA((FLOWS, samples)), pltpu.SemaphoreType.DMA((1 + len(w_post),))]
-    if near_part is not None:
-        scratch += [pltpu.SemaphoreType.DMA((2, 2, part_shape[1] // CHUNK))] * 2 + [pltpu.SemaphoreType.DMA((part_shape[1] // CHUNK,))] * 2
-    if far_src is not None:
+    if given(gate):
+        scratch.append(pltpu.VMEM((samples, rows, 1), jnp.float32))
+    if given(kv):
+        scratch += [pltpu.VMEM((2, 2) + kv[0].shape[1:], bf16), pltpu.VMEM((dim, 2 * kv[2].shape[1]), bf16), pltpu.SemaphoreType.DMA((2, 2)), pltpu.SemaphoreType.DMA((2,))]
+    scratch += [pltpu.SemaphoreType.DMA((FLOWS, samples)), pltpu.SemaphoreType.DMA((FLOWS, samples)), pltpu.SemaphoreType.DMA((2 + len(w_post),))]
+    if given(near_part):
+        scratch += [pltpu.SemaphoreType.DMA((2, 2, part_shape[1] // CHUNKS[near_part]))] * 2 + [pltpu.SemaphoreType.DMA((part_shape[1] // CHUNKS[near_part],))] * 2
+    if given(far_src):
         scratch += [pltpu.SemaphoreType.DMA] * 2
-    if aux is not None:
+    if given(aux):
         scratch += [pltpu.SemaphoreType.DMA((8,)), pltpu.SemaphoreType.DMA((8,))]
     return pl.pallas_call(
-        functools.partial(fused_kernel, samples, has_pre, has_post, mode, gate is not None, aux is not None, rope is not None, len(w_post), gain_row, near_part, far_src is not None),
+        functools.partial(fused_kernel, samples, has_pre, has_post, mode, gate[2] if given(gate) else None, given(aux), given(rope), len(w_post), gain_row, near_part, given(far_src), given(kv)),
         out_shape=tuple(outs), in_specs=specs, out_specs=tuple(out_specs),
         scratch_shapes=scratch, name=f'fused_{cid}',
         cost_estimate=pl.CostEstimate(flops=flops + 2 * 10 ** 10, bytes_accessed=10 ** 7, transcendentals=0),
@@ -454,9 +489,9 @@
 STAT = 8
 
 
-def cross_kernel(samples, n_w, q_ref, seen_ref, gain_ref, own_hbm, par_hbm, *refs):
+def cross_kernel(samples, n_w, q_ref, seen_ref, gain_ref, own_hbm, par_hbm, kv_hbm, *refs):
     w_hbm, refs = refs[:n_w], refs[n_w:]
-    ctx, q_all, w_vm, vis_vm, k_vm, v_vm, ob_l, ob_h, rec_x1, rec_y1, two_l, two_h, rec_y2, rec_x2, send, recv, wsem, vsem = refs
+    ctx, q_all, w_vm, vis_vm, kv_vm, k_vm, v_vm, ob_l, ob_h, rec_x1, rec_y1, two_l, two_h, rec_y2, rec_x2, send, recv, wsem, vsem, kv_sem = refs
     me = lax.axis_index('tp')
     z = lax.axis_index('dp')
     x = (me // 2) % 2
@@ -466,23 +501,24 @@
     vis_rows = own_hbm.shape[1]
     top, low = pl.ds(0, rows // 2), pl.ds(rows // 2, rows // 2)
     half = size // 2
-    scale = size ** -0.5
-    sources = [w_hbm[0], w_hbm[1]]
-    targets = [w_vm.at[0, :, pl.ds(0, size)], w_vm.at[0, :, pl.ds(size, size)]]
-    part = w_hbm[2].shape[2]
-    for i, ref in enumerate(w_hbm[2:]):
+    sources, targets = [], []
+    part = w_hbm[0].shape[2]
+    for i, ref in enumerate(w_hbm):
         base = part * (2 * (i // 2) + (z + i) % 2)
         for p in range(3):
             for kind in range(2):
                 sources.append(ref.at[p, kind])
-                targets.append(w_vm.at[1 + p, pl.ds(base, part), pl.ds(kind * size, size)])
+                targets.append(w_vm.at[p, pl.ds(base, part), pl.ds(kind * size, size)])
     loads = [pltpu.make_async_copy(src, dst, wsem.at[i]) for i, (src, dst) in enumerate(zip(sources, targets))]
 
     def vis_loads(s):
         spot = s % 2
         return [pltpu.make_async_copy(src.at[s], vis_vm.at[spot, i], vsem.at[spot, i]) for i, src in enumerate((own_hbm, par_hbm))]
 
-    for ld in vis_loads(0):
+    def kv_load(s):
+        return pltpu.make_async_copy(kv_hbm.at[s], kv_vm.at[s % 2], kv_sem.at[s % 2])
+
+    for ld in vis_loads(0) + [kv_load(0)]:
         ld.start()
     for ld in loads:
         ld.start()
@@ -550,16 +586,15 @@
         seen = seen_ref[s] > 0
         spot = s % 2
         for p in range(4):
-            cols = pl.ds(p * size, size)
-            keys = k_vm[spot, :, cols]
-            vals = v_vm[spot, :, cols]
-            scores = lax.dot_general(keys, near(q_all, s, p)[...], (((1,), (1,)), ((), ())), preferred_element_type=jnp.float32) * scale
-            scores = jnp.where(seen, scores, MASK_VALUE)
+            cols = pl.ds((p - 1) * size, size)
+            keys = k_vm[spot, :, cols] if p else kv_vm[spot, :, pl.ds(0, size)]
+            vals = v_vm[spot, :, cols] if p else kv_vm[spot, :, pl.ds(size, size)]
+            scores = lax.dot_general(keys, near(q_all, s, p)[...], (((1,), (1,)), ((), ())), preferred_element_type=jnp.float32)
             peak = jnp.max(scores, axis=0, keepdims=True)
             weights = jnp.exp(scores - peak)
             total = jnp.sum(weights, axis=0, keepdims=True)
             context = lax.dot_general(vals, weights.astype(jnp.bfloat16), (((0,), (0,)), ((), ())), preferred_element_type=jnp.float32)
-            stats = stat_block(peak, total)
+            stats = stat_block(jnp.where(seen, peak, MASK_VALUE), total)
             for ref, part in ((ob_l, context[:half]), (ob_h, context[half:])):
                 near(ref, s, p)[:half] = part
                 near(ref, s, p)[half:] = stats
@@ -600,13 +635,13 @@
 
         @pl.when(s + 1 < samples)
         def _():
-            for ld in vis_loads(s + 1):
+            for ld in vis_loads(s + 1) + [kv_load(s + 1)]:
                 ld.start()
-        for ld in vis_loads(s):
+        for ld in vis_loads(s) + [kv_load(s)]:
             ld.wait()
         spot = s % 2
         rows_in = vis_vm[spot].reshape(2 * vis_rows, -1)
-        for p in range(4):
+        for p in range(3):
             cols = pl.ds(p * size, size)
             keys = jnp.dot(rows_in, w_vm[p, :, pl.ds(0, size)], preferred_element_type=jnp.float32)
             mean_sq = jnp.mean(keys * keys, axis=-1, keepdims=True)
@@ -639,7 +674,7 @@
     lax.fori_loop(0, samples, drain, 0)
 
 
-def cross(cid, queries, seen, gain, own, partner, weights, tokens):
+def cross(cid, queries, seen, gain, own, partner, kv_own, weights, tokens):
     samples, rows, size = queries.shape
     vis_rows, dim = own.shape[1:]
     f32, bf16 = jnp.float32, jnp.bfloat16
@@ -648,22 +683,22 @@
     hbm = pl.BlockSpec(memory_space=pl.ANY)
     wide = pltpu.VMEM((samples, 2, half + STAT, rows), f32)
     one = pltpu.VMEM((samples, half + STAT, rows), f32)
-    both = pltpu.VMEM((samples, 2, 2, half + STAT, rows), f32)
-    heads = pltpu.VMEM((2, 2 * vis_rows, 4 * size), bf16)
+    both = pltpu.VMEM((samples, *PLANE, half + STAT, rows), f32)
+    heads = pltpu.VMEM((2, 2 * vis_rows, 3 * size), bf16)
     return pl.pallas_call(
         functools.partial(cross_kernel, samples, len(weights)),
         out_shape=jax.ShapeDtypeStruct((samples, tokens, rows // tokens * size), bf16),
-        in_specs=[vmem, vmem, vmem] + [hbm] * (2 + len(weights)), out_specs=vmem,
+        in_specs=[vmem, vmem, vmem] + [hbm] * (3 + len(weights)), out_specs=vmem,
         scratch_shapes=[
-            pltpu.VMEM((samples, 2, 2, rows, size), bf16), pltpu.VMEM((4, dim, 2 * size), bf16),
-            pltpu.VMEM((2, 2, vis_rows, dim), bf16), heads, heads,
+            pltpu.VMEM((samples, *PLANE, rows, size), bf16), pltpu.VMEM((3, dim, 2 * size), bf16),
+            pltpu.VMEM((2, 2, vis_rows, dim), bf16), pltpu.VMEM((2, 2 * vis_rows, 2 * size), bf16), heads, heads,
             both, both, wide, wide, wide, wide, one, one,
             pltpu.SemaphoreType.DMA((8, samples)), pltpu.SemaphoreType.DMA((8, samples)),
-            pltpu.SemaphoreType.DMA((26,)), pltpu.SemaphoreType.DMA((2, 2))],
+            pltpu.SemaphoreType.DMA((24,)), pltpu.SemaphoreType.DMA((2, 2)), pltpu.SemaphoreType.DMA((2,))],
         name=f'cross_{cid}',
         cost_estimate=pl.CostEstimate(flops=8 * 10 ** 10, bytes_accessed=10 ** 7, transcendentals=0),
         compiler_params=pltpu.CompilerParams(collective_id=cid, has_side_effects=True, vmem_limit_bytes=60 * 2 ** 20),
-    )(queries, seen, gain, own, partner, *weights)
+    )(queries, seen, gain, own, partner, kv_own, *weights)
 
 
 def solution(mesh):
@@ -683,8 +718,8 @@
         kv_local = wk_a.shape[1] // head_dim
         rep_heads = wq_a.shape[1] // head_dim // kv_local
 
-        gains = jnp.stack([ln1_a, ln2_a, ln1_b, ln2_b])
-        head_gains = jnp.stack([q_norm, k_norm])
+        gains = jnp.stack([g.astype(jnp.float32) for g in (ln1_a, ln2_a, ln1_b, ln2_b)])
+        head_gains = jnp.stack([q_norm.astype(jnp.float32), k_norm.astype(jnp.float32)])
         vis_partner = lax.ppermute(vision, 'tp', [(i, i ^ 1) for i in range(8)])
 
         small = jnp.concatenate([positions.reshape(-1), tile_mask.reshape(-1)])
@@ -697,13 +732,11 @@
         angles = pos_all.astype(jnp.float32)[..., None] * rope_table(head_dim)
         rope = (jnp.cos(angles), jnp.sin(angles))
         h_one, act, near_two, far_one = fused(2, hidden, lhs=proj, w_pre=wo_a, rope=rope, gain=gains, gain_row=1, w_post=(wg_a, wu_a), mode='swiglu', mine=(wk_b, wv_b), near_part=1, far_src=near_one)
-        h_two, queries, far_two = fused(3, h_one, lhs=act, w_pre=wd_a, gain=gains, gain_row=2, w_post=(wq_b,), mode='queries', q_gain=head_gains, far_src=near_two)
-        weights = (wk_b, wv_b, near_one, far_one, near_two, far_two)
+        h_two, queries, kv_own, far_two = fused(3, h_one, lhs=act, w_pre=wd_a, gain=gains, gain_row=2, w_post=(wq_b,), mode='queries', q_gain=head_gains, far_src=near_two, kv=(vision, vis_partner, wk_b, wv_b))
+        weights = (near_one, far_one, near_two, far_two)
         seen = jnp.tile(lax.dynamic_index_in_dim(mask_all, me // 2, axis=2, keepdims=False)[:, None, :], (1, 1, rep_heads))
-        context = cross(6, queries, seen, head_gains, vision, vis_partner, weights, tokens)
-        row_keep = jnp.any(tile_mask > 0, axis=-1, keepdims=True).astype(jnp.float32)
-        gate_vals = jnp.tanh(xgates.astype(jnp.float32))
-        h_three, act = fused(4, h_two, lhs=context, w_pre=wo_b, gate=gate_vals[0] * row_keep, gain=gains, gain_row=3, w_post=(wg_b, wu_b), mode='swiglu')
-        return fused(5, h_three, lhs=act, w_pre=wd_b, gate=gate_vals[1] * row_keep)[0]
+        context = cross(6, queries, seen, head_gains, vision, vis_partner, kv_own, weights, tokens)
+        h_three, act = fused(4, h_two, lhs=context, w_pre=wo_b, gate=(tile_mask, xgates, 0), gain=gains, gain_row=3, w_post=(wg_b, wu_b), mode='swiglu')
+        return fused(5, h_three, lhs=act, w_pre=wd_b, gate=(tile_mask, xgates, 1))[0]
 
     return jax.shard_map(body, mesh=mesh, in_specs=in_specs, out_specs=act_spec, check_vma=False)

time: 439 us -> 435 us (level)
  transfers between devices with their start and end apart: 1 -> 1, of which waited for: 0 -> 0; matrix products, arithmetic and copies ran while one was open for 4% -> 3% of each run, Pallas kernels for 51% -> 36%
where the time goes in v3:
time: 435 us; the launch traced here: 434 us
  Pallas kernels  415 us (95%)
  local copies, waits for them, and re-layouts  13.4 us (3%)
  other arithmetic  5.1 us (1%)
    pallas_call x5, Pallas kernels, fused(): pl.pallas_call(functools.partial(fused_kernel, samples, has_pre, has_post...  327 us
    pallas_call x1, Pallas kernels, cross(): pl.pallas_call(functools.partial(cross_kernel, samples, len(weights)), ou...  87.8 us
  transfers between devices with their start and end apart: 1, of which 0 were waited for; matrix products, arithmetic and copies ran while one was open for 3% of the time, Pallas kernels for 36%

profile of v3, /device:TPU:0, one launch (start us, length us, event | category | flops | bytes accessed | tf_op | source)
XLA Modules:
  0.0 434.0 jit_solution(123810910460901036)
XLA Ops:
  0.0 0.5 collective-permute-start
  0.5 0.8 reshape.35
  1.3 1.2 stack.40
  2.5 1.2 stack.41
  3.7 0.7 stack.34
  4.5 0.7 stack.35
  5.2 0.7 stack.36
  5.9 0.7 stack.37
  6.6 0.8 copy.35.refs_3_
  7.4 0.0 copy-start
  7.4 0.6 copy-done
  8.0 0.1 reshape.36
  8.1 0.1 pad_add_fusion
  8.2 0.6 pad_bitcast_fusion.refs_5_
  8.8 0.7 maximum_convert_fusion.refs_1_.refs_5_.refs_8_
  9.5 64.0 %fused_1.1 = (f32[6,128,1024]{2,1,0:T(8,128)}, s32[8,8,128]{2,1,0:T(8,128)}, bf16[3,2,896,256]{3,2,1,0:T(8,128)(2,1)}) custom-call(bf16[6,16,3584]{2,1,0:T(8,128)(2,1)} %refs_4_.5, f32[4,3584]{1,0:T(4,128)} %maximum_convert_fusion.refs_1_.refs_5_.refs_8_, bf16[3584,512]{1,0:T(8,128)(2,1)} %refs_2_.1, bf16[3584,256]{1,0:T(8,128)(2,1)} %refs_3_.4, ...), custom_call_target="tpu_custom_call" | custom-call | flops 25637144576 | bytes 10000000 | tf_op jit(solution)/shard_map/fused_1/pallas_call | solution.py:479
  73.6 0.8 copy.46
  74.3 0.1 slice.9
  74.4 0.1 convert_element_type.23
  74.5 0.1 convert_element_type.25
  74.6 0.1 copy.42
  74.7 0.1 copy.38
  74.8 0.1 reshape.40
  74.9 0.6 copy.47
  75.5 1.2 maximum_convert_fusion.1.refs_2_.gain_ref
  76.7 3.1 multiply_sine_fusion
  79.9 90.5 %fused_2.1 = (bf16[6,16,3584]{2,1,0:T(8,128)(2,1)}, bf16[6,128,1792]{2,1,0:T(8,128)(2,1)}, bf16[3,2,896,256]{3,2,1,0:T(8,128)(2,1)}, bf16[3,2,896,256]{3,2,1,0:T(8,128)(2,1)}) custom-call(f32[6,128,1024]{2,1,0:T(8,128)} %get-tuple-element.18.refs_0_, bf16[512,3584]{1,0:T(8,128)(2,1)} %refs_1_.4, f32[6,128,128]{2,1,0:T(8,128)} %get-tuple-element.32.refs_2_, ...), custom_call_target="tpu_custom_call" | custom-call | flops 42548576256 | bytes 10000000 | tf_op jit(solution)/shard_map/fused_2/pallas_call | solution.py:479
  170.3 0.0 collective-permute-done.refs_4_.par_hbm
  170.3 68.3 %fused_3.1 = (bf16[6,16,3584]{2,1,0:T(8,128)(2,1)}, bf16[6,256,256]{2,1,0:T(8,128)(2,1)}, bf16[6,512,512]{2,1,0:T(8,128)(2,1)}, bf16[3,2,896,256]{3,2,1,0:T(8,128)(2,1)}) custom-call(bf16[6,128,1792]{2,1,0:T(8,128)(2,1)} %get-tuple-element.21.refs_0_, bf16[1792,3584]{1,0:T(8,128)(2,1)} %refs_1_.5, f32[2,256]{1,0:T(2,128)} %maximum_convert_fusion.1.refs_2_.gain_ref, ...), custom_call_target="tpu_custom_call" | custom-call | flops 32683575296 | bytes 10000000 | tf_op jit(solution)/shard_map/fused_3/pallas_call | solution.py:479
  238.7 1.3 tile.11
  239.9 87.8 %cross_6.1.refs_0_ = bf16[6,128,512]{2,1,0:T(8,128)(2,1)} custom-call(bf16[6,256,256]{2,1,0:T(8,128)(2,1)} %get-tuple-element.24.q_ref, s32[6,1,256]{2,1,0:T(1,128)} %bitcast.24, f32[2,256]{1,0:T(2,128)} %maximum_convert_fusion.1.refs_2_.gain_ref, bf16[6,256,3584]{2,1,0:T(8,128)(2,1)} %own_hbm.1, bf16[6,256,3584]{2,1,0:T(8,128)(2,1)} %collective-permute-done.refs_4_.par_hbm, ...), custom_call_target="tpu_custom_call" | custom-call | flops 80000000000 | bytes 10000000 | tf_op jit(solution)/shard_map/cross_6/pallas_call | solution.py:688
  327.7 65.4 %fused_4.1 = (bf16[6,16,3584]{2,1,0:T(8,128)(2,1)}, bf16[6,128,1792]{2,1,0:T(8,128)(2,1)}) custom-call(bf16[6,128,512]{2,1,0:T(8,128)(2,1)} %cross_6.1.refs_0_, bf16[512,3584]{1,0:T(8,128)(2,1)} %refs_1_.6, bf16[6,16,3584]{2,1,0:T(8,128)(2,1)} %get-tuple-element.28.refs_2_, s32[6,16,4]{2,1,0:T(8,128)} %copy-done, f32[2]{0:T(128)} %refs_4_.7, ...), custom_call_target="tpu_custom_call" | custom-call | flops 42548576256 | bytes 10000000 | tf_op jit(solution)/shard_map/fused_4/pallas_call | solution.py:479
  393.1 38.9 %fused_5.1 = bf16[6,16,3584]{2,1,0:T(8,128)(2,1)} custom-call(bf16[6,128,1792]{2,1,0:T(8,128)(2,1)} %get-tuple-element.29.refs_0_, bf16[1792,3584]{1,0:T(8,128)(2,1)} %refs_1_.7, bf16[6,16,3584]{2,1,0:T(8,128)(2,1)} %get-tuple-element.30.refs_2_, s32[6,16,4]{2,1,0:T(8,128)} %copy-done, f32[2]{0:T(128)} %refs_4_.7), custom_call_target="tpu_custom_call" | custom-call | flops 29865003008 | bytes 10000000 | tf_op jit(solution)/shard_map/fused_5/pallas_call | solution.py:479
  432.0 2.0 copy.49
  (3 shorter events, 0.0 us)
Async XLA Ops:
  0.0 170.3 %collective-permute-start = (bf16[6,256,3584]{2,1,0:T(8,128)(2,1)}, bf16[6,256,3584]{2,1,0:T(8,128)(2,1)}, u32[]{:S(2)}, u32[]{:S(2)}) collective-permute-start(bf16[6,256,3584]{2,1,0:T(8,128)(2,1)} %own_hbm.1), channel_id=1, source_target_pairs={{0,1},{1,0},{2,3},{3,2},{4,5},{5,4},{6,7},{7,6},{8,9},{9,8},{10,11... | collective-permute-start | bytes 33030152 | tf_op jit(solution)/shard_map/ppermute | solution.py:723
  7.4 0.6 copy-start
